TPU v7x, 256 devices: a whole 4x4x8 slice. The times are simulated.
256 devices in a mesh: graph: 64 (over z, y, core), feat: 4 (over x).
Axes of the slice: x: 4, y: 4, z: 8, core: 2. Of those that a mesh axis runs over, the one named last changes fastest.
Arguments:
- node_feats: bfloat16 [20480, 512], P(('graph', 'feat')), may hold values from -6 to 6
- edge_feats: bfloat16 [131072, 512], P(('graph', 'feat')), may hold values from -6 to 6
- senders: int32 [131072], P(('graph', 'feat')), may hold values from 0 to 319
- receiver_ref: int32 [131072], P(('graph', 'feat')), may hold values from 0 to 6463, as said below
- send_list: int32 [64, 64, 96], P('graph'), may hold values from 0 to 319, as said below
- edge_count: int32 [64], P('graph'), may hold values from 1024 to 2048, as said below
- edge_w1: bfloat16 [1536, 512], replicated, may hold values from -0.15625 to 0.15625
- edge_w2: bfloat16 [512, 512], replicated, may hold values from -0.25 to 0.25
- edge_gain: bfloat16 [512], replicated, may hold values from 0.099609375 to 1.8984375
- edge_shift: bfloat16 [512], replicated, may hold values from -3 to 3
- node_w1: bfloat16 [1024, 512], replicated, may hold values from -0.1875 to 0.1875
- node_w2: bfloat16 [512, 512], replicated, may hold values from -0.25 to 0.25
- node_gain: bfloat16 [512], replicated, may hold values from 0.099609375 to 1.8984375
- node_shift: bfloat16 [512], replicated, may hold values from -3 to 3
Outputs:
- new_edges: bfloat16 [131072, 512], P(('graph', 'feat'))
- new_nodes: bfloat16 [20480, 512], P(('graph', 'feat'))
Inputs may be any that keep to these rules, and one draw needn't show every extreme that they name: `senders`: local node indices of the edge's own region. `receiver_ref`: A value below 320 is a node of the edge's own region. Otherwise q = value - 320 names slot q % 96 of the list that region s = q // 96 keeps for the edge's region; s is never the edge's own region, and when s is more than 2 steps away around the region order (either direction, wrapping) the slot is below 16. In every draw each region has an edge on slot 95 of the next region and an edge on slot 15 of the region 3 steps on. Each list send_list[s, g] holds 96 distinct local node indices of region s. Region g's live edges are its first edge_count[g] edge slots; some region has all 2048 live.
All inputs are finite; a program needn't handle non-finite values.
Results may differ from a plain program's by a relative error of at most 0.009.
Values may be sent and summed in bfloat16 or wider, within the bound.
A program may use at most 128 MiB of HBM per device.

v0:
```python
import jax
import jax.numpy as jnp
from jax import lax
from jax.sharding import PartitionSpec as P

NODE_DEV = 320
SLOT = 96
FAR_SLOT = 16
REACH = 2


epsilon = 1e-05


def in_order(tiles, dim):
    dims = list(tiles.shape[1:])
    dims[dim] *= tiles.shape[0]
    return jnp.moveaxis(tiles, 0, dim).reshape(dims)


def copy_for_each(value, axis):
    devices = lax.axis_size(axis)
    return lax.all_to_all(
        jnp.broadcast_to(value[None], (devices, *value.shape)), axis, 0, 0, tiled=True
    )


def gathered_copies(value, axis, dim):
    return in_order(copy_for_each(value, axis), dim)


def passed_along(value, axis, by):
    devices = lax.axis_size(axis)
    return lax.ppermute(value, axis, [(i, (i + by) % devices) for i in range(devices)])


def cut_along(value, dim, devices):
    before, after = (value.shape[:dim], value.shape[dim + 1 :])
    return jnp.moveaxis(value.reshape(*before, devices, -1, *after), dim, 0)


def sum_at_owner(value, axis, dim):
    tiles = cut_along(value, dim, lax.axis_size(axis))
    arrived = lax.all_to_all(tiles, axis, split_axis=0, concat_axis=0, tiled=True)
    return arrived.astype(jnp.float32).sum(axis=0)


def layer_norm(outputs, norm_gain, norm_shift):
    average = jnp.mean(outputs, axis=-1, keepdims=True)
    centered = outputs - average
    variance = jnp.mean(centered * centered, axis=-1, keepdims=True)
    return centered * lax.rsqrt(variance + epsilon) * norm_gain + norm_shift


def perceptron(inputs, first_weight, second_weight, norm_gain, norm_shift):
    joined = jnp.concatenate(inputs, axis=1)
    activation = jnp.dot(joined, first_weight, preferred_element_type=jnp.float32)
    hidden = jax.nn.silu(activation).astype(jnp.bfloat16)
    outputs = jnp.dot(hidden, second_weight, preferred_element_type=jnp.float32)
    return layer_norm(outputs, norm_gain, norm_shift)


def one_hot_rows(indices, width):
    return (indices[:, None] == lax.iota(jnp.int32, width)[None, :]).astype(jnp.bfloat16)


def sum_into(selector, values):
    return lax.dot_general(
        selector, values, (((0,), (0,)), ((), ())), preferred_element_type=jnp.float32
    )


def per_device(
    node_feats,
    edge_feats,
    senders,
    receiver_ref,
    send_list,
    edge_count,
    edge_w1,
    edge_w2,
    edge_gain,
    edge_shift,
    node_w1,
    node_w2,
    node_gain,
    node_shift,
):
    feature_width = node_feats.shape[1]
    edge_local = edge_feats.shape[0]
    groups = lax.axis_size("graph")
    own_index = lax.axis_index("graph")
    share_index = lax.axis_index("feat")
    region_nodes = gathered_copies(node_feats, "feat", 0)
    send_rows = send_list[0]
    pieces = 1
    part_index = 0
    quarter = SLOT // pieces
    far_count = FAR_SLOT // pieces
    my_rows = lax.dynamic_index_in_dim(
        send_rows.reshape(groups, quarter, pieces), part_index, 2, keepdims=False
    ).reshape(-1)
    list_select = one_hot_rows(my_rows, NODE_DEV)
    outgoing = (
        jnp.dot(list_select, region_nodes, preferred_element_type=jnp.float32)
        .astype(jnp.bfloat16)
        .reshape(groups, quarter, feature_width)
    )
    offsets = [distance for distance in range(-REACH, REACH + 1) if distance != 0]
    far_part = lax.all_to_all(
        outgoing[:, :far_count], "graph", split_axis=0, concat_axis=0, tiled=True
    )
    received = jnp.pad(far_part, ((0, 0), (0, quarter - far_count), (0, 0)))
    for distance in offsets:
        near_block = lax.dynamic_index_in_dim(
            outgoing, (own_index - distance) % groups, 0, keepdims=False
        )
        arrived = passed_along(near_block, "graph", -distance)
        received = lax.dynamic_update_index_in_dim(
            received, arrived, (own_index + distance) % groups, 0
        )
    offset = jnp.maximum(receiver_ref - NODE_DEV, 0)
    source = offset // SLOT
    slot_index = offset % SLOT
    arranged = source * SLOT + slot_index % pieces * quarter + slot_index // pieces
    row_index = jnp.where(receiver_ref < NODE_DEV, receiver_ref, NODE_DEV + arranged)
    table_rows = NODE_DEV + groups * SLOT
    table = jnp.concatenate([region_nodes, received.reshape(groups * SLOT, feature_width)], axis=0)
    receiver_select = one_hot_rows(row_index, table_rows)
    sender_select = one_hot_rows(senders, NODE_DEV)
    sender_rows = jnp.dot(sender_select, region_nodes, preferred_element_type=jnp.float32).astype(
        jnp.bfloat16
    )
    receiver_rows = jnp.dot(receiver_select, table, preferred_element_type=jnp.float32).astype(
        jnp.bfloat16
    )
    update = edge_feats.astype(jnp.float32) + perceptron(
        (edge_feats, sender_rows, receiver_rows), edge_w1, edge_w2, edge_gain, edge_shift
    )
    live_mask = share_index * edge_local + lax.iota(jnp.int32, edge_local) < edge_count[0]
    new_edges = jnp.where(live_mask[:, None], update, edge_feats.astype(jnp.float32)).astype(
        jnp.bfloat16
    )
    messages = jnp.where(live_mask[:, None], new_edges, jnp.zeros_like(new_edges))
    segment_totals = sum_into(receiver_select, messages)
    own_sums = segment_totals[:NODE_DEV]
    partial_value = segment_totals[NODE_DEV:].reshape(groups, SLOT, feature_width)
    far_back = lax.all_to_all(
        partial_value[:, :far_count].astype(jnp.bfloat16),
        "graph",
        split_axis=0,
        concat_axis=0,
        tiled=True,
    ).astype(jnp.float32)
    returned = jnp.pad(far_back, ((0, 0), (0, quarter - far_count), (0, 0)))
    for distance in offsets:
        near_block = lax.dynamic_index_in_dim(
            partial_value, (own_index + distance) % groups, 0, keepdims=False
        )
        arrived = passed_along(near_block.astype(jnp.bfloat16), "graph", distance).astype(
            near_block.dtype
        )
        returned = lax.dynamic_update_index_in_dim(
            returned, arrived, (own_index - distance) % groups, 0
        )
    flat_returned = returned.reshape(groups * quarter, feature_width)
    upper_part = flat_returned.astype(jnp.bfloat16)
    lower_part = (flat_returned - upper_part.astype(jnp.float32)).astype(jnp.bfloat16)
    listed_sums = sum_into(list_select, upper_part) + sum_into(list_select, lower_part)
    node_sums = sum_at_owner((own_sums + listed_sums).astype(jnp.bfloat16), "feat", 0)
    aggregate = node_sums.astype(jnp.bfloat16)
    node_update = node_feats.astype(jnp.float32) + perceptron(
        (node_feats, aggregate), node_w1, node_w2, node_gain, node_shift
    )
    return (new_edges, node_update.astype(jnp.bfloat16))


def solution(mesh):
    return jax.shard_map(
        per_device,
        mesh=mesh,
        in_specs=(
            P(("graph", "feat"), None),
            P(("graph", "feat"), None),
            P(("graph", "feat")),
            P(("graph", "feat")),
            P("graph", None, None),
            P("graph"),
            P(),
            P(),
            P(),
            P(),
            P(),
            P(),
            P(),
            P(),
        ),
        out_specs=(P(("graph", "feat"), None), P(("graph", "feat"), None)),
        check_vma=False,
    )
```

profile of v0, /device:TPU:1, one launch (start us, length us, event | category | flops | bytes accessed | tf_op | source)
XLA Modules:
  0.0 173.4 jit_solution(17367850225809019450)
XLA Ops:
  0.6 1.8 %broadcast_in_dim.77 = bf16[4,80,512]{2,1,0:T(8,128)(2,1)} broadcast(bf16[80,512]{1,0:T(8,128)(2,1)} %param.14), dimensions={1,2} | broadcast | bytes 409600 | tf_op jit(solution)/shard_map/broadcast_in_dim | solution.py:24
  2.4 4.8 %all-to-all-start = ((bf16[4,80,512]{2,1,0:T(8,128)(2,1)}), bf16[4,80,512]{2,1,0:T(8,128)(2,1)S(1)}, u32[]{:S(2)}, u32[]{:S(2)}) async-start(bf16[4,80,512]{2,1,0:T(8,128)(2,1)} %broadcast_in_dim.77), calls=%async_computation | async-start | bytes 655360 | tf_op jit(solution)/shard_map/all_to_all | solution.py:23
  8.1 5.0 %all-to-all-done = bf16[4,80,512]{2,1,0:T(8,128)(2,1)S(1)} async-done(((bf16[4,80,512]{2,1,0:T(8,128)(2,1)}), bf16[4,80,512]{2,1,0:T(8,128)(2,1)S(1)}, u32[]{:S(2)}, u32[]{:S(2)}) %all-to-all-start) | async-done | bytes 327712 | tf_op jit(solution)/shard_map/all_to_all | solution.py:23
  13.1 3.7 %convolution_convert_fusion = bf16[6144,512]{1,0:T(8,128)(2,1)S(1)} fusion(bf16[320,512]{1,0:T(8,128)(2,1)S(1)} %bitcast.62, s32[6144]{0:T(1024)S(1)} %eq.67), kind=kOutput, calls=%fused_computation.6 | convolution fusion | flops 2018377728 | bytes 6643712 | tf_op jit(solution)/shard_map/dot_general | solution.py:105
  16.9 2.7 %copy-done.5 = bf16[6144,512]{1,0:T(8,128)(2,1)} copy-done((bf16[6144,512]{1,0:T(8,128)(2,1)}, bf16[6144,512]{1,0:T(8,128)(2,1)S(1)}, u32[]{:S(2)}) %copy-start.5) | copy-done | bytes 6291480
  20.6 14.1 %all-to-all-start.1 = ((bf16[64,16,512]{2,1,0:T(8,128)(2,1)}), bf16[64,16,512]{2,1,0:T(8,128)(2,1)S(1)}, u32[]{:S(2)}, u32[]{:S(2)}) async-start(bf16[64,16,512]{2,1,0:T(8,128)(2,1)} %slice.17), calls=%async_computation.1 | async-start | bytes 2097152 | tf_op jit(solution)/shard_map/all_to_all | solution.py:110
  36.8 1.8 %dynamic-slice_bitcast_fusion = (bf16[96,512]{1,0:T(8,128)(2,1)}, bf16[96,512]{1,0:T(8,128)(2,1)}, bf16[96,512]{1,0:T(8,128)(2,1)}, bf16[96,512]{1,0:T(8,128)(2,1)}) fusion(bf16[64,96,512]{2,1,0:T(8,128)(2,1)} %bitcast.61, s32[]{:T(128)S(6)} %select_n.104, s32[]{:T(128)S(6)} %select_n.108, s32[]{:T(128)S(6)} %select_n.106, s32[]{:T(128)S(6)} %select_n.102), kind=kLoop, calls=%fused_computation.67 | loop fusion | bytes 786448 | tf_op jit(solution)/shard_map/jit(dynamic_index_in_dim)/squeeze | solution.py:115
  41.7 3.6 %collective-permute-start.3 = (bf16[96,512]{1,0:T(8,128)(2,1)}, bf16[96,512]{1,0:T(8,128)(2,1)}, u32[]{:S(2)}, u32[]{:S(2)}) collective-permute-start(bf16[96,512]{1,0:T(8,128)(2,1)} %get-tuple-element.12), channel_id=1, source_target_pairs={{0,248},{4,252},{8,0},{12,4},{16,8},{20,12},{24,16},{28,20},{32,24... | collective-permute-start | bytes 294920 | tf_op jit(solution)/shard_map/ppermute | solution.py:34
  46.5 17.8 %all-to-all-done.1 = bf16[64,16,512]{2,1,0:T(8,128)(2,1)S(1)} async-done(((bf16[64,16,512]{2,1,0:T(8,128)(2,1)}), bf16[64,16,512]{2,1,0:T(8,128)(2,1)S(1)}, u32[]{:S(2)}, u32[]{:S(2)}) %all-to-all-start.1) | async-done | bytes 1048608 | tf_op jit(solution)/shard_map/all_to_all | solution.py:110
  68.8 4.5 %fusion.21 = bf16[512,512]{1,0:T(8,128)(2,1)} fusion(bf16[6144,512]{1,0:T(8,128)(2,1)S(1)} %bitcast.59, bf16[320,512]{1,0:T(8,128)(2,1)S(1)} %bitcast.64, s32[512]{0:T(512)S(1)} %compare_select_fusion), kind=kOutput, calls=%fused_computation.28 | convolution fusion | flops 3405807616 | bytes 7145472 | tf_op jit(solution)/shard_map/dot_general | solution.py:134
  73.3 3.1 %fusion.65 = (f32[512]{0:T(512)S(1)}, f32[512,512]{0,1:T(8,128)S(1)}) fusion(bf16[512,512]{1,0:T(8,128)(2,1)} %param.21, bf16[1536,512]{1,0:T(8,128)(2,1)S(1)} %copy-done, bf16[512,512]{1,0:T(8,128)(2,1)} %fusion.21, bf16[512,512]{1,0:T(8,128)(2,1)} %convolution_convert_fusion.1, bf16[512,512]{1,0:T(8,128)(2,1)} %param.15), kind=kOutput, calls=%fused_computation.93 | convolution fusion | flops 1080032768 | bytes 4720640 | tf_op jit(solution)/shard_map/dot_general | solution.py:59
  76.9 7.1 %fusion.5 = f32[6464,512]{1,0:T(8,128)} fusion(s32[512]{0:T(512)S(1)} %compare_select_fusion, bf16[512,512]{0,1:T(8,128)(2,1)S(1)} %fusion.27, pred[512]{0:T(512)(128)(4,1)S(1)} %add_compare_fusion), kind=kOutput, calls=%fused_computation.10 | convolution fusion | flops 3395878912 | bytes 13765120 | tf_op jit(solution)/shard_map/dot_general | solution.py:68
  84.0 8.0 %slice.19 = bf16[6144,512]{1,0:T(8,128)(2,1)} slice(f32[6464,512]{1,0:T(8,128)} %fusion.5), slice={[320:6464], [0:512]} | slice | bytes 12582912 | tf_op jit(solution)/shard_map/slice | solution.py:147
  92.0 2.3 %slice.23 = bf16[64,16,512]{2,1,0:T(8,128)(2,1)} slice(bf16[64,96,512]{2,1,0:T(8,128)(2,1)} %bitcast.57), slice={[0:64], [0:16], [0:512]} | slice | bytes 2097152 | tf_op jit(solution)/shard_map/slice | solution.py:149
  94.3 6.0 %all-to-all-start.2 = ((bf16[64,16,512]{2,1,0:T(8,128)(2,1)}), bf16[64,16,512]{2,1,0:T(8,128)(2,1)S(1)}, u32[]{:S(2)}, u32[]{:S(2)}) async-start(bf16[64,16,512]{2,1,0:T(8,128)(2,1)} %slice.23), calls=%async_computation.2 | async-start | bytes 2097152 | tf_op jit(solution)/shard_map/all_to_all | solution.py:148
  101.3 5.1 %collective-permute-start.4 = (bf16[96,512]{1,0:T(8,128)(2,1)S(1)}, bf16[96,512]{1,0:T(8,128)(2,1)S(1)}, u32[]{:S(2)}, u32[]{:S(2)}) collective-permute-start(bf16[96,512]{1,0:T(8,128)(2,1)S(1)} %get-tuple-element.11), channel_id=1, source_target_pairs={{0,248},{4,252},{8,0},{12,4},{16,8},{20,12},{24,16},{28,20},{32,24... | collective-permute-start | bytes 294920 | tf_op jit(solution)/shard_map/ppermute | solution.py:34
  108.1 21.8 %all-to-all-done.2 = bf16[64,16,512]{2,1,0:T(8,128)(2,1)S(1)} async-done(((bf16[64,16,512]{2,1,0:T(8,128)(2,1)}), bf16[64,16,512]{2,1,0:T(8,128)(2,1)S(1)}, u32[]{:S(2)}, u32[]{:S(2)}) %all-to-all-start.2) | async-done | bytes 1048608 | tf_op jit(solution)/shard_map/all_to_all | solution.py:148
  129.9 6.2 %pad_convert_fusion = f32[64,96,512]{2,1,0:T(8,128)} fusion(bf16[64,16,512]{2,1,0:T(8,128)(2,1)S(1)} %all-to-all-done.2), kind=kLoop, calls=%fused_computation.16 | loop fusion | flops 3145728 | bytes 13631488 | tf_op jit(solution)/shard_map/jit(_pad)/pad | solution.py:155
  138.9 11.1 %fusion.2 = (bf16[6144,512]{1,0:T(8,128)(2,1)}, bf16[6144,512]{1,0:T(8,128)(2,1)}) fusion(f32[64,96,512]{2,1,0:T(8,128)} %convert_dynamic-update-slice_fusion), kind=kLoop, calls=%fused_computation.5 | loop fusion | flops 12582912 | bytes 25165824 | tf_op jit(solution)/shard_map/convert_element_type | solution.py:168
  149.9 5.1 %fusion.3 = f32[320,512]{1,0:T(8,128)S(1)} fusion(bf16[6144,512]{1,0:T(8,128)(2,1)} %get-tuple-element.6, s32[6144]{0:T(1024)S(1)} %eq.67), kind=kOutput, calls=%fused_computation.8 | convolution fusion | flops 2015232000 | bytes 6971392 | tf_op jit(solution)/shard_map/dot_general | solution.py:68
  155.2 4.2 %fusion.26 = bf16[320,512]{1,0:T(8,128)(2,1)} fusion(f32[320,512]{1,0:T(8,128)S(1)} %fusion.3, bf16[6144,512]{1,0:T(8,128)(2,1)S(1)} %copy-done.2, s32[6144]{0:T(1024)S(1)} %eq.67, f32[6464,512]{1,0:T(8,128)} %fusion.5), kind=kOutput, calls=%fused_computation.32 | convolution fusion | flops 2015723520 | bytes 7954432 | tf_op jit(solution)/shard_map/dot_general | solution.py:68
  159.3 3.5 %all-to-all-start.3 = ((bf16[4,80,512]{2,1,0:T(8,128)(2,1)}), bf16[4,80,512]{2,1,0:T(8,128)(2,1)S(1)}, u32[]{:S(2)}, u32[]{:S(2)}) async-start(bf16[4,80,512]{2,1,0:T(8,128)(2,1)} %bitcast.22), calls=%async_computation.3 | async-start | bytes 655360 | tf_op jit(solution)/shard_map/all_to_all | solution.py:44
  163.8 6.7 %all-to-all-done.3 = bf16[4,80,512]{2,1,0:T(8,128)(2,1)S(1)} async-done(((bf16[4,80,512]{2,1,0:T(8,128)(2,1)}), bf16[4,80,512]{2,1,0:T(8,128)(2,1)S(1)}, u32[]{:S(2)}, u32[]{:S(2)}) %all-to-all-start.3) | async-done | bytes 327712 | tf_op jit(solution)/shard_map/all_to_all | solution.py:44
  170.6 1.8 %fusion.68 = (f32[80]{0:T(128)S(1)}, f32[80,512]{1,0:T(8,128)S(1)}) fusion(bf16[512,512]{1,0:T(8,128)(2,1)S(1)} %copy-done.12, bf16[1024,512]{1,0:T(8,128)(2,1)} %param.24, bf16[80,512]{1,0:T(8,128)(2,1)S(1)} %reduce_sum.50, bf16[80,512]{1,0:T(8,128)(2,1)S(1)} %copy-done.6), kind=kOutput, calls=%fused_computation.94 | convolution fusion | flops 126402480 | bytes 1900864 | tf_op jit(solution)/shard_map/dot_general | solution.py:59
  (71 shorter events, 20.2 us)
Async XLA Ops:
  0.6 72.7 %copy-start = (bf16[1536,512]{1,0:T(8,128)(2,1)S(1)}, bf16[1536,512]{1,0:T(8,128)(2,1)}, u32[]{:S(2)}) copy-start(bf16[1536,512]{1,0:T(8,128)(2,1)} %param.20) | copy-start | bytes 4718596
  2.4 10.7 %all-to-all-start = ((bf16[4,80,512]{2,1,0:T(8,128)(2,1)}), bf16[4,80,512]{2,1,0:T(8,128)(2,1)S(1)}, u32[]{:S(2)}, u32[]{:S(2)}) async-start(bf16[4,80,512]{2,1,0:T(8,128)(2,1)} %broadcast_in_dim.77), calls=%async_computation | async-start | bytes 655360 | tf_op jit(solution)/shard_map/all_to_all | solution.py:23
  13.1 23.6 %copy-start.8 = (bf16[512]{0:T(512)(128)(2,1)S(1)}, bf16[512]{0:T(512)(128)(2,1)}, u32[]{:S(2)}) copy-start(bf16[512]{0:T(512)(128)(2,1)} %param.22) | copy-start | bytes 3076
  13.1 23.6 %copy-start.9 = (bf16[512]{0:T(512)(128)(2,1)S(1)}, bf16[512]{0:T(512)(128)(2,1)}, u32[]{:S(2)}) copy-start(bf16[512]{0:T(512)(128)(2,1)} %param.23) | copy-start | bytes 3076
  13.1 23.6 %copy-start.7 = (s32[512]{0:T(512)S(1)}, s32[512]{0:T(512)}, u32[]{:S(2)}) copy-start(s32[512]{0:T(512)} %param.17) | copy-start | bytes 6148
  13.1 32.2 %copy-start.13 = (s32[512]{0:T(512)S(1)}, s32[512]{0:T(512)}, u32[]{:S(2)}) copy-start(s32[512]{0:T(512)} %param.16) | copy-start | bytes 6148
  20.6 43.7 %all-to-all-start.1 = ((bf16[64,16,512]{2,1,0:T(8,128)(2,1)}), bf16[64,16,512]{2,1,0:T(8,128)(2,1)S(1)}, u32[]{:S(2)}, u32[]{:S(2)}) async-start(bf16[64,16,512]{2,1,0:T(8,128)(2,1)} %slice.17), calls=%async_computation.1 | async-start | bytes 2097152 | tf_op jit(solution)/shard_map/all_to_all | solution.py:110
  38.6 26.6 %collective-permute-start = (bf16[96,512]{1,0:T(8,128)(2,1)}, bf16[96,512]{1,0:T(8,128)(2,1)}, u32[]{:S(2)}, u32[]{:S(2)}) collective-permute-start(bf16[96,512]{1,0:T(8,128)(2,1)} %get-tuple-element.15), channel_id=1, source_target_pairs={{0,8},{4,12},{8,16},{12,20},{16,24},{20,28},{24,32},{28,36},{32,40... | collective-permute-start | bytes 294920 | tf_op jit(solution)/shard_map/ppermute | solution.py:34
  39.9 26.1 %collective-permute-start.1 = (bf16[96,512]{1,0:T(8,128)(2,1)}, bf16[96,512]{1,0:T(8,128)(2,1)}, u32[]{:S(2)}, u32[]{:S(2)}) collective-permute-start(bf16[96,512]{1,0:T(8,128)(2,1)} %get-tuple-element.14), channel_id=1, source_target_pairs={{0,4},{4,8},{8,12},{12,16},{16,20},{20,24},{24,28},{28,32},{32,36}... | collective-permute-start | bytes 294920 | tf_op jit(solution)/shard_map/ppermute | solution.py:34
  41.7 25.3 %collective-permute-start.2 = (bf16[96,512]{1,0:T(8,128)(2,1)}, bf16[96,512]{1,0:T(8,128)(2,1)}, u32[]{:S(2)}, u32[]{:S(2)}) collective-permute-start(bf16[96,512]{1,0:T(8,128)(2,1)} %get-tuple-element.13), channel_id=1, source_target_pairs={{0,252},{4,0},{8,4},{12,8},{16,12},{20,16},{24,20},{28,24},{32,28}... | collective-permute-start | bytes 294920 | tf_op jit(solution)/shard_map/ppermute | solution.py:34
  41.7 26.2 %collective-permute-start.3 = (bf16[96,512]{1,0:T(8,128)(2,1)}, bf16[96,512]{1,0:T(8,128)(2,1)}, u32[]{:S(2)}, u32[]{:S(2)}) collective-permute-start(bf16[96,512]{1,0:T(8,128)(2,1)} %get-tuple-element.12), channel_id=1, source_target_pairs={{0,248},{4,252},{8,0},{12,4},{16,8},{20,12},{24,16},{28,20},{32,24... | collective-permute-start | bytes 294920 | tf_op jit(solution)/shard_map/ppermute | solution.py:34
  76.9 7.1 %copy-start.3 = (bf16[512,512]{0,1:T(8,128)(2,1)}, bf16[512,512]{0,1:T(8,128)(2,1)S(1)}, u32[]{:S(2)}) copy-start(bf16[512,512]{0,1:T(8,128)(2,1)S(1)} %fusion.27) | copy-start | bytes 1572868
  94.3 35.6 %all-to-all-start.2 = ((bf16[64,16,512]{2,1,0:T(8,128)(2,1)}), bf16[64,16,512]{2,1,0:T(8,128)(2,1)S(1)}, u32[]{:S(2)}, u32[]{:S(2)}) async-start(bf16[64,16,512]{2,1,0:T(8,128)(2,1)} %slice.23), calls=%async_computation.2 | async-start | bytes 2097152 | tf_op jit(solution)/shard_map/all_to_all | solution.py:148
  101.3 34.8 %collective-permute-start.4 = (bf16[96,512]{1,0:T(8,128)(2,1)S(1)}, bf16[96,512]{1,0:T(8,128)(2,1)S(1)}, u32[]{:S(2)}, u32[]{:S(2)}) collective-permute-start(bf16[96,512]{1,0:T(8,128)(2,1)S(1)} %get-tuple-element.11), channel_id=1, source_target_pairs={{0,248},{4,252},{8,0},{12,4},{16,8},{20,12},{24,16},{28,20},{32,24... | collective-permute-start | bytes 294920 | tf_op jit(solution)/shard_map/ppermute | solution.py:34
  106.4 30.4 %collective-permute-start.5 = (bf16[96,512]{1,0:T(8,128)(2,1)S(1)}, bf16[96,512]{1,0:T(8,128)(2,1)S(1)}, u32[]{:S(2)}, u32[]{:S(2)}) collective-permute-start(bf16[96,512]{1,0:T(8,128)(2,1)S(1)} %get-tuple-element.10), channel_id=1, source_target_pairs={{0,252},{4,0},{8,4},{12,8},{16,12},{20,16},{24,20},{28,24},{32,28}... | collective-permute-start | bytes 294920 | tf_op jit(solution)/shard_map/ppermute | solution.py:34
  107.0 30.4 %collective-permute-start.6 = (bf16[96,512]{1,0:T(8,128)(2,1)S(1)}, bf16[96,512]{1,0:T(8,128)(2,1)S(1)}, u32[]{:S(2)}, u32[]{:S(2)}) collective-permute-start(bf16[96,512]{1,0:T(8,128)(2,1)S(1)} %get-tuple-element.9), channel_id=1, source_target_pairs={{0,4},{4,8},{8,12},{12,16},{16,20},{20,24},{24,28},{28,32},{32,36}... | collective-permute-start | bytes 294920 | tf_op jit(solution)/shard_map/ppermute | solution.py:34
  108.1 30.0 %collective-permute-start.7 = (bf16[96,512]{1,0:T(8,128)(2,1)S(1)}, bf16[96,512]{1,0:T(8,128)(2,1)S(1)}, u32[]{:S(2)}, u32[]{:S(2)}) collective-permute-start(bf16[96,512]{1,0:T(8,128)(2,1)S(1)} %get-tuple-element.8), channel_id=1, source_target_pairs={{0,8},{4,12},{8,16},{12,20},{16,24},{20,28},{24,32},{28,36},{32,40... | collective-permute-start | bytes 294920 | tf_op jit(solution)/shard_map/ppermute | solution.py:34
  155.1 7.7 %copy-start.10 = (bf16[512]{0:T(512)(128)(2,1)S(1)}, bf16[512]{0:T(512)(128)(2,1)}, u32[]{:S(2)}) copy-start(bf16[512]{0:T(512)(128)(2,1)} %param.26) | copy-start | bytes 3076
  155.1 7.7 %copy-start.11 = (bf16[512]{0:T(512)(128)(2,1)S(1)}, bf16[512]{0:T(512)(128)(2,1)}, u32[]{:S(2)}) copy-start(bf16[512]{0:T(512)(128)(2,1)} %param.27) | copy-start | bytes 3076
  155.1 7.7 %copy-start.4 = (bf16[512,512]{0,1:T(8,128)(2,1)S(1)}, bf16[512,512]{0,1:T(8,128)(2,1)}, u32[]{:S(2)}) copy-start(bf16[512,512]{0,1:T(8,128)(2,1)} %copy-done.3) | copy-start | bytes 1572868
  155.1 15.5 %copy-start.6 = (bf16[80,512]{1,0:T(8,128)(2,1)S(1)}, bf16[80,512]{1,0:T(8,128)(2,1)}, u32[]{:S(2)}) copy-start(bf16[80,512]{1,0:T(8,128)(2,1)} %param.14) | copy-start | bytes 245764
  155.1 15.5 %copy-start.12 = (bf16[512,512]{1,0:T(8,128)(2,1)S(1)}, bf16[512,512]{1,0:T(8,128)(2,1)}, u32[]{:S(2)}) copy-start(bf16[512,512]{1,0:T(8,128)(2,1)} %param.25) | copy-start | bytes 1572868
  155.1 18.3 %copy-start.1 = (bf16[1536,512]{1,0:T(8,128)(2,1)S(1)}, bf16[1536,512]{1,0:T(8,128)(2,1)}, u32[]{:S(2)}) copy-start(bf16[1536,512]{1,0:T(8,128)(2,1)} %param.20) | copy-start | bytes 4718596
  159.3 11.2 %all-to-all-start.3 = ((bf16[4,80,512]{2,1,0:T(8,128)(2,1)}), bf16[4,80,512]{2,1,0:T(8,128)(2,1)S(1)}, u32[]{:S(2)}, u32[]{:S(2)}) async-start(bf16[4,80,512]{2,1,0:T(8,128)(2,1)} %bitcast.22), calls=%async_computation.3 | async-start | bytes 655360 | tf_op jit(solution)/shard_map/all_to_all | solution.py:44
  (2 other events, 7.8 us)
where the time goes:
time: 174 us; the launch traced here: 173 us
  waiting for transfers between devices  51.3 us (29%)
  starting transfers between devices  41.8 us (24%)
  matrix products  30.8 us (18%)
  local copies, waits for them, and re-layouts  26.2 us (15%)
  other arithmetic  21.6 us (12%)
    all_to_all x1, waiting for transfers between devices, per_device(): lax.all_to_all(partial_value[:, :far_count].astype(jnp.bfloat16), 'graph'...  21.8 us
    all_to_all x1, waiting for transfers between devices, per_device(): lax.all_to_all(outgoing[:, :far_count], 'graph', split_axis=0, concat_axi...  17.8 us
    dot_general x3, matrix products, sum_into(): lax.dot_general(selector, values, (((0,), (0,)), ((), ())), preferred_ele...  16.4 us
    all_to_all x1, starting transfers between devices, per_device(): lax.all_to_all(outgoing[:, :far_count], 'graph', split_axis=0, concat_axi...  14.1 us
    ppermute x8, starting transfers between devices, passed_along(): lax.ppermute(value, axis, [(i, (i + by) % devices) for i in range(devices)])  13.5 us
    convert_element_type x1, other arithmetic, per_device(): (flat_returned - upper_part.astype(jnp.float32)).astype(jnp.bfloat16)  11.1 us
    slice x1, local copies, waits for them, and re-layouts, per_device(): segment_totals[NODE_DEV:].reshape(groups, SLOT, feature_width)  7.98 us
    all_to_all x1, waiting for transfers between devices, sum_at_owner(): lax.all_to_all(tiles, axis, split_axis=0, concat_axis=0, tiled=True)  6.71 us
  transfers between devices with their start and end apart: 12, of which 4 were waited for; matrix products, arithmetic and copies ran while one was open for 11% of the time, Pallas kernels for 0%

commit v1 on v0

v1 whole, which is shorter than its diff:
```python
import jax
import jax.numpy as jnp
from jax import lax
from jax.sharding import PartitionSpec as P

NODE_DEV = 320
SLOT = 96
FAR_SLOT = 16
REACH = 2
OFFSETS = (-2, -1, 1, 2)


epsilon = 1e-05


def layer_norm(outputs, norm_gain, norm_shift):
    average = jnp.mean(outputs, axis=-1, keepdims=True)
    centered = outputs - average
    variance = jnp.mean(centered * centered, axis=-1, keepdims=True)
    return centered * lax.rsqrt(variance + epsilon) * norm_gain + norm_shift


def perceptron(inputs, first_weight, second_weight, norm_gain, norm_shift):
    joined = jnp.concatenate(inputs, axis=1)
    activation = jnp.dot(joined, first_weight, preferred_element_type=jnp.float32)
    hidden = jax.nn.silu(activation).astype(jnp.bfloat16)
    outputs = jnp.dot(hidden, second_weight, preferred_element_type=jnp.float32)
    return layer_norm(outputs, norm_gain, norm_shift)


def one_hot_rows(indices, width):
    return (indices[:, None] == lax.iota(jnp.int32, width)[None, :]).astype(jnp.bfloat16)


def pick(selector, values):
    return jnp.dot(selector, values, preferred_element_type=jnp.float32).astype(jnp.bfloat16)


def sum_into(selector, values):
    return lax.dot_general(
        selector, values, (((0,), (0,)), ((), ())), preferred_element_type=jnp.float32
    )


def exchange(tiles, axis):
    return lax.all_to_all(tiles, axis, split_axis=0, concat_axis=0, tiled=True)


def passed_along(value, axis, by):
    devices = lax.axis_size(axis)
    return lax.ppermute(value, axis, [(i, (i + by) % devices) for i in range(devices)])


def everywhere(value, axis):
    devices = lax.axis_size(axis)
    return exchange(jnp.broadcast_to(value[None], (devices, *value.shape)), axis)


def quarters(value, parts):
    rows, width = value.shape
    return jnp.moveaxis(value.reshape(rows, parts, width // parts), 1, 0)


def rejoined(tiles):
    parts, rows, width = tiles.shape
    return jnp.moveaxis(tiles, 0, 1).reshape(rows, parts * width)


def per_device(
    node_feats,
    edge_feats,
    senders,
    receiver_ref,
    send_list,
    edge_count,
    edge_w1,
    edge_w2,
    edge_gain,
    edge_shift,
    node_w1,
    node_w2,
    node_gain,
    node_shift,
):
    width = node_feats.shape[1]
    edge_local = edge_feats.shape[0]
    groups = lax.axis_size("graph")
    parts = lax.axis_size("feat")
    own = lax.axis_index("graph")
    share = lax.axis_index("feat")
    quarter = width // parts
    far_rows = groups * FAR_SLOT
    table_rows = far_rows + len(OFFSETS) * SLOT

    region_nodes = everywhere(node_feats, "feat").reshape(NODE_DEV, width)
    all_refs = everywhere(receiver_ref[None], "feat").reshape(-1)
    my_nodes = lax.dynamic_slice_in_dim(region_nodes, share * quarter, quarter, 1)

    send_rows = send_list[0]
    near_lists = [
        lax.dynamic_index_in_dim(send_rows, (own + d) % groups, 0, keepdims=False) for d in OFFSETS
    ]
    out_rows = jnp.concatenate([send_rows[:, :FAR_SLOT].reshape(-1), *near_lists])
    list_select = one_hot_rows(out_rows, NODE_DEV)
    outgoing = pick(list_select, my_nodes)
    far_part = exchange(outgoing[:far_rows].reshape(groups, FAR_SLOT, quarter), "graph")
    near_part = []
    for n, d in enumerate(OFFSETS):
        block = outgoing[far_rows + n * SLOT : far_rows + (n + 1) * SLOT]
        near_part.append(passed_along(block, "graph", d))
    table = jnp.concatenate([far_part.reshape(far_rows, quarter), *near_part])

    offset = jnp.maximum(all_refs - NODE_DEV, 0)
    source = offset // SLOT
    slot = offset % SLOT
    row = source * FAR_SLOT + slot
    for n, d in enumerate(OFFSETS):
        row = jnp.where(source == (own - d) % groups, far_rows + n * SLOT + slot, row)
    row = jnp.where(all_refs < NODE_DEV, -1, row)
    own_row = jnp.where(all_refs < NODE_DEV, all_refs, -1)
    table_select = one_hot_rows(row, table_rows)

    picked = pick(table_select, table).reshape(parts, edge_local, quarter)
    away_rows = rejoined(exchange(picked, "feat"))
    sender_rows = pick(one_hot_rows(senders, NODE_DEV), region_nodes)
    local_rows = pick(one_hot_rows(receiver_ref, NODE_DEV), region_nodes)
    receiver_rows = local_rows + away_rows

    update = edge_feats.astype(jnp.float32) + perceptron(
        (edge_feats, sender_rows, receiver_rows), edge_w1, edge_w2, edge_gain, edge_shift
    )
    live = share * edge_local + lax.iota(jnp.int32, edge_local) < edge_count[0]
    new_edges = jnp.where(live[:, None], update, edge_feats.astype(jnp.float32)).astype(
        jnp.bfloat16
    )
    messages = jnp.where(live[:, None], new_edges, jnp.zeros_like(new_edges))
    arrived = exchange(quarters(messages, parts), "feat").reshape(parts * edge_local, quarter)
    away_sums = sum_into(table_select, arrived).astype(jnp.bfloat16)
    own_sums = sum_into(one_hot_rows(own_row, NODE_DEV), arrived)
    far_back = exchange(away_sums[:far_rows].reshape(groups, FAR_SLOT, quarter), "graph")
    near_back = []
    for n, d in enumerate(OFFSETS):
        block = away_sums[far_rows + n * SLOT : far_rows + (n + 1) * SLOT]
        near_back.append(passed_along(block, "graph", -d))
    returned = jnp.concatenate([far_back.reshape(far_rows, quarter), *near_back])
    totals = (own_sums + sum_into(list_select, returned)).astype(jnp.bfloat16)
    aggregate = rejoined(exchange(totals.reshape(parts, NODE_DEV // parts, quarter), "feat"))
    node_update = node_feats.astype(jnp.float32) + perceptron(
        (node_feats, aggregate), node_w1, node_w2, node_gain, node_shift
    )
    return (new_edges, node_update.astype(jnp.bfloat16))


def solution(mesh):
    return jax.shard_map(
        per_device,
        mesh=mesh,
        in_specs=(
            P(("graph", "feat"), None),
            P(("graph", "feat"), None),
            P(("graph", "feat")),
            P(("graph", "feat")),
            P("graph", None, None),
            P("graph"),
            P(),
            P(),
            P(),
            P(),
            P(),
            P(),
            P(),
            P(),
        ),
        out_specs=(P(("graph", "feat"), None), P(("graph", "feat"), None)),
        check_vma=False,
    )
```

time: 174 us -> 122 us (0.70)
  waiting for transfers between devices: 51.3 us -> 27.9 us
  other arithmetic: 21.6 us -> 3.4 us
  local copies, waits for them, and re-layouts: 26.2 us -> 9.7 us
  matrix products: 30.8 us -> 17.3 us
  blocking collectives: 0 us -> 10.7 us
  starting transfers between devices: 41.8 us -> 50.7 us
    all_to_all x4 -> x6, waiting for transfers between devices: 51.3 us -> 27.8 us  [exchange(): return lax.all_to_all(tiles, axis, split_axis=0, concat_axis=0, tiled=True)]
    convert_element_type x2 -> x0, other arithmetic: 11.4 us -> none  [the longest x1 11.1 us: per_device(): (flat_returned - upper_part.astype(jnp.float32)).astype(jnp.bfloat16)]
    all_to_all x0 -> x1, blocking collectives: none -> 10.7 us  [exchange(): return lax.all_to_all(tiles, axis, split_axis=0, concat_axis=0, tiled=True)]
    dot_general x3, matrix products: 16.4 us -> 6.44 us  [sum_into(): lax.dot_general(selector, values, (((0,), (0,)), ((), ())), preferred_ele...]
    slice x3 -> x4, local copies, waits for them, and re-layouts: 11.3 us -> 1.46 us  [the longest x1 0.72 us: per_device(): outgoing[:far_rows].reshape(groups, FAR_SLOT, quarter)]
    all_to_all x4 -> x6, starting transfers between devices: 28.3 us -> 37.1 us  [exchange(): return lax.all_to_all(tiles, axis, split_axis=0, concat_axis=0, tiled=True)]
    pad x1 -> x0, other arithmetic: 6.2 us -> none  [per_device(): returned = jnp.pad(far_back, ((0, 0), (0, quarter - far_count), (0, 0)))]
    dynamic_update_slice x4 -> x0, local copies, waits for them, and re-layouts: 3.63 us -> none  [per_device(): lax.dynamic_update_index_in_dim(received, arrived, (own_index + distance)...]
  transfers between devices with their start and end apart: 12 -> 14, of which waited for: 4 -> 7; matrix products, arithmetic and copies ran while one was open for 11% -> 6% of each run, Pallas kernels for 0% -> 0%
where the time goes in v1:
time: 122 us; the launch traced here: 121 us
  starting transfers between devices  50.7 us (42%)
  waiting for transfers between devices  27.9 us (23%)
  matrix products  17.3 us (14%)
  blocking collectives  10.7 us (9%)
  local copies, waits for them, and re-layouts  9.7 us (8%)
  other arithmetic  3.4 us (3%)
  between operations  1.6 us (1%)
    all_to_all x6, starting transfers between devices, exchange(): return lax.all_to_all(tiles, axis, split_axis=0, concat_axis=0, tiled=True)  37.1 us
    all_to_all x6, waiting for transfers between devices, exchange(): return lax.all_to_all(tiles, axis, split_axis=0, concat_axis=0, tiled=True)  27.8 us
    ppermute x8, starting transfers between devices, passed_along(): lax.ppermute(value, axis, [(i, (i + by) % devices) for i in range(devices)])  13.6 us
    all_to_all x1, blocking collectives, exchange(): return lax.all_to_all(tiles, axis, split_axis=0, concat_axis=0, tiled=True)  10.7 us
    dot_general x3, matrix products, sum_into(): lax.dot_general(selector, values, (((0,), (0,)), ((), ())), preferred_ele...  6.44 us
    dot_general x4, matrix products, pick(): jnp.dot(selector, values, preferred_element_type=jnp.float32)  6.12 us
    dot_general x2, matrix products, perceptron(): outputs = jnp.dot(hidden, second_weight, preferred_element_type=jnp.float32)  4.71 us
    broadcast_in_dim x2, local copies, waits for them, and re-layouts, everywhere(): jnp.broadcast_to(value[None], (devices, *value.shape))  3.04 us
  transfers between devices with their start and end apart: 14, of which 7 were waited for; matrix products, arithmetic and copies ran while one was open for 6% of the time, Pallas kernels for 0%

profile of v1, /device:TPU:1, one launch (start us, length us, event | category | flops | bytes accessed | tf_op | source)
XLA Modules:
  0.0 121.3 jit_solution(4698450074130246952)
XLA Ops:
  0.6 1.8 %broadcast_in_dim.21 = bf16[4,80,512]{2,1,0:T(8,128)(2,1)} broadcast(bf16[80,512]{1,0:T(8,128)(2,1)} %param.14), dimensions={1,2} | broadcast | bytes 409600 | tf_op jit(solution)/shard_map/broadcast_in_dim | solution.py:56
  2.4 4.8 %all-to-all-start = ((bf16[4,80,512]{2,1,0:T(8,128)(2,1)}), bf16[4,80,512]{2,1,0:T(8,128)(2,1)S(1)}, u32[]{:S(2)}, u32[]{:S(2)}) async-start(bf16[4,80,512]{2,1,0:T(8,128)(2,1)} %broadcast_in_dim.21), calls=%async_computation | async-start | bytes 655360 | tf_op jit(solution)/shard_map/all_to_all | solution.py:46
  8.9 4.2 %all-to-all-done = bf16[4,80,512]{2,1,0:T(8,128)(2,1)S(1)} async-done(((bf16[4,80,512]{2,1,0:T(8,128)(2,1)}), bf16[4,80,512]{2,1,0:T(8,128)(2,1)S(1)}, u32[]{:S(2)}, u32[]{:S(2)}) %all-to-all-start) | async-done | bytes 327712 | tf_op jit(solution)/shard_map/all_to_all | solution.py:46
  14.4 3.2 %all-to-all-start.1 = ((s32[4,1,512]{2,1,0:T(1,128)}), s32[4,1,512]{2,1,0:T(1,128)S(1)}, u32[]{:S(2)}, u32[]{:S(2)}) async-start(s32[4,1,512]{2,1,0:T(1,128)} %broadcast_in_dim.22), calls=%async_computation.1 | async-start | bytes 16384 | tf_op jit(solution)/shard_map/all_to_all | solution.py:46
  19.0 2.8 %all-to-all-done.1 = s32[4,1,512]{2,1,0:T(1,128)S(1)} async-done(((s32[4,1,512]{2,1,0:T(1,128)}), s32[4,1,512]{2,1,0:T(1,128)S(1)}, u32[]{:S(2)}, u32[]{:S(2)}) %all-to-all-start.1) | async-done | bytes 8224 | tf_op jit(solution)/shard_map/all_to_all | solution.py:46
  21.8 15.2 %all-to-all-start.2 = ((bf16[64,16,128]{2,1,0:T(8,128)(2,1)}), bf16[64,16,128]{2,1,0:T(8,128)(2,1)S(1)}, u32[]{:S(2)}, u32[]{:S(2)}) async-start(bf16[64,16,128]{2,1,0:T(8,128)(2,1)} %bitcast.8), calls=%async_computation.2 | async-start | bytes 524288 | tf_op jit(solution)/shard_map/all_to_all | solution.py:46
  37.1 5.1 %collective-permute-start = (bf16[96,128]{1,0:T(8,128)(2,1)S(1)}, bf16[96,128]{1,0:T(8,128)(2,1)S(1)}, u32[]{:S(2)}, u32[]{:S(2)}) collective-permute-start(bf16[96,128]{1,0:T(8,128)(2,1)S(1)} %get-tuple-element.15), channel_id=1, source_target_pairs={{0,248},{4,252},{8,0},{12,4},{16,8},{20,12},{24,16},{28,20},{32,24... | collective-permute-start | bytes 73736 | tf_op jit(solution)/shard_map/ppermute | solution.py:51
  43.9 6.2 %all-to-all-done.2 = bf16[64,16,128]{2,1,0:T(8,128)(2,1)S(1)} async-done(((bf16[64,16,128]{2,1,0:T(8,128)(2,1)}), bf16[64,16,128]{2,1,0:T(8,128)(2,1)S(1)}, u32[]{:S(2)}, u32[]{:S(2)}) %all-to-all-start.2) | async-done | bytes 262176 | tf_op jit(solution)/shard_map/all_to_all | solution.py:46
  50.3 3.0 %fusion.5 = bf16[2048,128]{1,0:T(8,128)(2,1)} fusion(bf16[1408,128]{1,0:T(8,128)(2,1)S(1)} %constant_dynamic-update-slice_fusion, s32[2048]{0:T(1024)S(1)} %get-tuple-element.21), kind=kOutput, calls=%fused_computation.7 | convolution fusion | flops 741343232 | bytes 892928 | tf_op jit(solution)/shard_map/dot_general | solution.py:36
  53.3 3.6 %all-to-all-start.3 = ((bf16[4,512,128]{2,1,0:T(8,128)(2,1)}), bf16[4,512,128]{2,1,0:T(8,128)(2,1)S(1)}, u32[]{:S(2)}, u32[]{:S(2)}) async-start(bf16[4,512,128]{2,1,0:T(8,128)(2,1)} %bitcast.10), calls=%async_computation.3 | async-start | bytes 1048576 | tf_op jit(solution)/shard_map/all_to_all | solution.py:46
  59.9 6.1 %all-to-all-done.3 = bf16[4,512,128]{2,1,0:T(8,128)(2,1)S(1)} async-done(((bf16[4,512,128]{2,1,0:T(8,128)(2,1)}), bf16[4,512,128]{2,1,0:T(8,128)(2,1)S(1)}, u32[]{:S(2)}, u32[]{:S(2)}) %all-to-all-start.3) | async-done | bytes 524320 | tf_op jit(solution)/shard_map/all_to_all | solution.py:46
  67.4 2.9 %fusion.55 = (f32[512]{0:T(512)S(1)}, f32[512,512]{0,1:T(8,128)S(1)}) fusion(bf16[512,512]{1,0:T(8,128)(2,1)} %param.21, bf16[1536,512]{1,0:T(8,128)(2,1)S(1)} %copy-done, bf16[512,512]{1,0:T(8,128)(2,1)} %fusion.15, bf16[512,512]{1,0:T(8,128)(2,1)} %convolution_convert_fusion.2, bf16[512,512]{1,0:T(8,128)(2,1)S(1)} %copy-done.1), kind=kOutput, calls=%fused_computation.85 | convolution fusion | flops 1080032768 | bytes 4720640 | tf_op jit(solution)/shard_map/dot_general | solution.py:27
  70.5 2.2 %broadcast_select_fusion = (bf16[512,512]{0,1:T(8,128)(2,1)}, bf16[512,512]{0,1:T(8,128)(2,1)S(1)}) fusion(pred[512]{0:T(512)(128)(4,1)S(1)} %add_compare_fusion, f32[512]{0:T(512)S(1)} %convert_element_type.61, f32[512]{0:T(512)S(1)} %convert_element_type.60, f32[512]{0:T(512)S(1)} %add_rsqrt_fusion, f32[512,512]{0,1:T(8,128)S(1)} %get-tuple-element.23, ...), kind=kLoop, calls=%fused_computation.34 | loop fusion | flops 2359296 | bytes 2630144 | tf_op jit(solution)/shard_map/jit(_where)/select_n | solution.py:136
  74.0 10.7 %all_to_all.35 = bf16[4,512,128]{2,1,0:T(8,128)(2,1)S(1)} all-to-all(bf16[4,512,128]{2,1,0:T(8,128)(2,1)S(1)} %bitcast.45), channel_id=1, replica_groups=mesh['graph'=64,'feat'=4] {'feat'}, dimensions={0} | all-to-all | bytes 1048576 | tf_op jit(solution)/shard_map/all_to_all | solution.py:46
  84.7 3.5 %fusion.6 = bf16[1408,128]{1,0:T(8,128)(2,1)S(1)} fusion(bf16[2048,128]{1,0:T(8,128)(2,1)S(1)} %bitcast.49, s32[2048]{0:T(1024)S(1)} %get-tuple-element.21), kind=kOutput, calls=%fused_computation.8 | convolution fusion | flops 741261312 | bytes 892928 | tf_op jit(solution)/shard_map/dot_general | solution.py:40
  88.9 6.9 %all-to-all-start.5 = ((bf16[64,16,128]{2,1,0:T(8,128)(2,1)}), bf16[64,16,128]{2,1,0:T(8,128)(2,1)S(1)}, u32[]{:S(2)}, u32[]{:S(2)}) async-start(bf16[64,16,128]{2,1,0:T(8,128)(2,1)} %bitcast.15), calls=%async_computation.5 | async-start | bytes 524288 | tf_op jit(solution)/shard_map/all_to_all | solution.py:46
  95.9 1.4 %collective-permute-start.4 = (bf16[96,128]{1,0:T(8,128)(2,1)S(1)}, bf16[96,128]{1,0:T(8,128)(2,1)S(1)}, u32[]{:S(2)}, u32[]{:S(2)}) collective-permute-start(bf16[96,128]{1,0:T(8,128)(2,1)S(1)} %get-tuple-element.11), channel_id=1, source_target_pairs={{0,8},{4,12},{8,16},{12,20},{16,24},{20,28},{24,32},{28,36},{32,40... | collective-permute-start | bytes 73736 | tf_op jit(solution)/shard_map/ppermute | solution.py:51
  97.3 1.7 %collective-permute-start.5 = (bf16[96,128]{1,0:T(8,128)(2,1)S(1)}, bf16[96,128]{1,0:T(8,128)(2,1)S(1)}, u32[]{:S(2)}, u32[]{:S(2)}) collective-permute-start(bf16[96,128]{1,0:T(8,128)(2,1)S(1)} %get-tuple-element.10), channel_id=1, source_target_pairs={{0,4},{4,8},{8,12},{12,16},{16,20},{20,24},{24,28},{28,32},{32,36}... | collective-permute-start | bytes 73736 | tf_op jit(solution)/shard_map/ppermute | solution.py:51
  99.1 3.6 %collective-permute-start.7 = (bf16[96,128]{1,0:T(8,128)(2,1)S(1)}, bf16[96,128]{1,0:T(8,128)(2,1)S(1)}, u32[]{:S(2)}, u32[]{:S(2)}) collective-permute-start(bf16[96,128]{1,0:T(8,128)(2,1)S(1)} %get-tuple-element.8), channel_id=1, source_target_pairs={{0,248},{4,252},{8,0},{12,4},{16,8},{20,12},{24,16},{28,20},{32,24... | collective-permute-start | bytes 73736 | tf_op jit(solution)/shard_map/ppermute | solution.py:51
  104.0 4.9 %all-to-all-done.5 = bf16[64,16,128]{2,1,0:T(8,128)(2,1)S(1)} async-done(((bf16[64,16,128]{2,1,0:T(8,128)(2,1)}), bf16[64,16,128]{2,1,0:T(8,128)(2,1)S(1)}, u32[]{:S(2)}, u32[]{:S(2)}) %all-to-all-start.5) | async-done | bytes 262176 | tf_op jit(solution)/shard_map/all_to_all | solution.py:46
  109.1 1.6 %fusion.17 = bf16[320,128]{1,0:T(8,128)(2,1)} fusion(f32[320,128]{1,0:T(8,128)S(1)} %fusion.4, bf16[1408,128]{1,0:T(8,128)(2,1)S(1)} %constant_dynamic-update-slice_fusion.5, s32[1408]{0:T(1024)S(1)} %concatenate.15), kind=kOutput, calls=%fused_computation.24 | convolution fusion | flops 115875840 | bytes 611840 | tf_op jit(solution)/shard_map/dot_general | solution.py:40
  110.7 3.3 %all-to-all-start.6 = ((bf16[4,80,128]{2,1,0:T(8,128)(2,1)}), bf16[4,80,128]{2,1,0:T(8,128)(2,1)S(1)}, u32[]{:S(2)}, u32[]{:S(2)}) async-start(bf16[4,80,128]{2,1,0:T(8,128)(2,1)} %bitcast.17), calls=%async_computation.6 | async-start | bytes 163840 | tf_op jit(solution)/shard_map/all_to_all | solution.py:46
  115.0 3.5 %all-to-all-done.6 = bf16[4,80,128]{2,1,0:T(8,128)(2,1)S(1)} async-done(((bf16[4,80,128]{2,1,0:T(8,128)(2,1)}), bf16[4,80,128]{2,1,0:T(8,128)(2,1)S(1)}, u32[]{:S(2)}, u32[]{:S(2)}) %all-to-all-start.6) | async-done | bytes 81952 | tf_op jit(solution)/shard_map/all_to_all | solution.py:46
  118.5 1.8 %fusion.58 = (f32[80]{0:T(128)S(1)}, f32[80,512]{1,0:T(8,128)S(1)}) fusion(bf16[512,512]{1,0:T(8,128)(2,1)S(1)} %copy-done.8, bf16[1024,512]{1,0:T(8,128)(2,1)} %param.24, bf16[80,512]{1,0:T(8,128)(2,1)S(1)} %copy_bitcast_fusion, bf16[80,512]{1,0:T(8,128)(2,1)S(1)} %copy-done.2), kind=kOutput, calls=%fused_computation.86 | convolution fusion | flops 126402480 | bytes 1900864 | tf_op jit(solution)/shard_map/dot_general | solution.py:27
  (71 shorter events, 15.5 us)
Async XLA Ops:
  0.6 66.7 %copy-start = (bf16[1536,512]{1,0:T(8,128)(2,1)S(1)}, bf16[1536,512]{1,0:T(8,128)(2,1)}, u32[]{:S(2)}) copy-start(bf16[1536,512]{1,0:T(8,128)(2,1)} %param.20) | copy-start | bytes 4718596
  2.4 10.7 %all-to-all-start = ((bf16[4,80,512]{2,1,0:T(8,128)(2,1)}), bf16[4,80,512]{2,1,0:T(8,128)(2,1)S(1)}, u32[]{:S(2)}, u32[]{:S(2)}) async-start(bf16[4,80,512]{2,1,0:T(8,128)(2,1)} %broadcast_in_dim.21), calls=%async_computation | async-start | bytes 655360 | tf_op jit(solution)/shard_map/all_to_all | solution.py:46
  14.4 7.4 %all-to-all-start.1 = ((s32[4,1,512]{2,1,0:T(1,128)}), s32[4,1,512]{2,1,0:T(1,128)S(1)}, u32[]{:S(2)}, u32[]{:S(2)}) async-start(s32[4,1,512]{2,1,0:T(1,128)} %broadcast_in_dim.22), calls=%async_computation.1 | async-start | bytes 16384 | tf_op jit(solution)/shard_map/all_to_all | solution.py:46
  21.8 28.3 %all-to-all-start.2 = ((bf16[64,16,128]{2,1,0:T(8,128)(2,1)}), bf16[64,16,128]{2,1,0:T(8,128)(2,1)S(1)}, u32[]{:S(2)}, u32[]{:S(2)}) async-start(bf16[64,16,128]{2,1,0:T(8,128)(2,1)} %bitcast.8), calls=%async_computation.2 | async-start | bytes 524288 | tf_op jit(solution)/shard_map/all_to_all | solution.py:46
  37.1 13.1 %collective-permute-start = (bf16[96,128]{1,0:T(8,128)(2,1)S(1)}, bf16[96,128]{1,0:T(8,128)(2,1)S(1)}, u32[]{:S(2)}, u32[]{:S(2)}) collective-permute-start(bf16[96,128]{1,0:T(8,128)(2,1)S(1)} %get-tuple-element.15), channel_id=1, source_target_pairs={{0,248},{4,252},{8,0},{12,4},{16,8},{20,12},{24,16},{28,20},{32,24... | collective-permute-start | bytes 73736 | tf_op jit(solution)/shard_map/ppermute | solution.py:51
  42.1 8.0 %collective-permute-start.1 = (bf16[96,128]{1,0:T(8,128)(2,1)S(1)}, bf16[96,128]{1,0:T(8,128)(2,1)S(1)}, u32[]{:S(2)}, u32[]{:S(2)}) collective-permute-start(bf16[96,128]{1,0:T(8,128)(2,1)S(1)} %get-tuple-element.14), channel_id=1, source_target_pairs={{0,252},{4,0},{8,4},{12,8},{16,12},{20,16},{24,20},{28,24},{32,28}... | collective-permute-start | bytes 73736 | tf_op jit(solution)/shard_map/ppermute | solution.py:51
  42.8 7.4 %collective-permute-start.2 = (bf16[96,128]{1,0:T(8,128)(2,1)S(1)}, bf16[96,128]{1,0:T(8,128)(2,1)S(1)}, u32[]{:S(2)}, u32[]{:S(2)}) collective-permute-start(bf16[96,128]{1,0:T(8,128)(2,1)S(1)} %get-tuple-element.13), channel_id=1, source_target_pairs={{0,4},{4,8},{8,12},{12,16},{16,20},{20,24},{24,28},{28,32},{32,36}... | collective-permute-start | bytes 73736 | tf_op jit(solution)/shard_map/ppermute | solution.py:51
  43.9 6.4 %collective-permute-start.3 = (bf16[96,128]{1,0:T(8,128)(2,1)S(1)}, bf16[96,128]{1,0:T(8,128)(2,1)S(1)}, u32[]{:S(2)}, u32[]{:S(2)}) collective-permute-start(bf16[96,128]{1,0:T(8,128)(2,1)S(1)} %get-tuple-element.12), channel_id=1, source_target_pairs={{0,8},{4,12},{8,16},{12,20},{16,24},{20,28},{24,32},{28,36},{32,40... | collective-permute-start | bytes 73736 | tf_op jit(solution)/shard_map/ppermute | solution.py:51
  50.3 7.3 %copy-start.1 = (bf16[512,512]{1,0:T(8,128)(2,1)S(1)}, bf16[512,512]{1,0:T(8,128)(2,1)}, u32[]{:S(2)}) copy-start(bf16[512,512]{1,0:T(8,128)(2,1)} %param.15) | copy-start | bytes 1572868
  53.3 5.3 %copy-start.4 = (bf16[512]{0:T(512)(128)(2,1)S(1)}, bf16[512]{0:T(512)(128)(2,1)}, u32[]{:S(2)}) copy-start(bf16[512]{0:T(512)(128)(2,1)} %param.22) | copy-start | bytes 3076
  53.3 5.3 %copy-start.5 = (bf16[512]{0:T(512)(128)(2,1)S(1)}, bf16[512]{0:T(512)(128)(2,1)}, u32[]{:S(2)}) copy-start(bf16[512]{0:T(512)(128)(2,1)} %param.23) | copy-start | bytes 3076
  53.3 5.3 %copy-start.9 = (s32[512]{0:T(512)S(1)}, s32[512]{0:T(512)}, u32[]{:S(2)}) copy-start(s32[512]{0:T(512)} %param.16) | copy-start | bytes 6148
  53.3 12.8 %copy-start.3 = (s32[512]{0:T(512)S(1)}, s32[512]{0:T(512)}, u32[]{:S(2)}) copy-start(s32[512]{0:T(512)} %param.17) | copy-start | bytes 6148
  53.3 12.8 %all-to-all-start.3 = ((bf16[4,512,128]{2,1,0:T(8,128)(2,1)}), bf16[4,512,128]{2,1,0:T(8,128)(2,1)S(1)}, u32[]{:S(2)}, u32[]{:S(2)}) async-start(bf16[4,512,128]{2,1,0:T(8,128)(2,1)} %bitcast.10), calls=%async_computation.3 | async-start | bytes 1048576 | tf_op jit(solution)/shard_map/all_to_all | solution.py:46
  88.9 20.0 %all-to-all-start.5 = ((bf16[64,16,128]{2,1,0:T(8,128)(2,1)}), bf16[64,16,128]{2,1,0:T(8,128)(2,1)S(1)}, u32[]{:S(2)}, u32[]{:S(2)}) async-start(bf16[64,16,128]{2,1,0:T(8,128)(2,1)} %bitcast.15), calls=%async_computation.5 | async-start | bytes 524288 | tf_op jit(solution)/shard_map/all_to_all | solution.py:46
  95.9 13.1 %collective-permute-start.4 = (bf16[96,128]{1,0:T(8,128)(2,1)S(1)}, bf16[96,128]{1,0:T(8,128)(2,1)S(1)}, u32[]{:S(2)}, u32[]{:S(2)}) collective-permute-start(bf16[96,128]{1,0:T(8,128)(2,1)S(1)} %get-tuple-element.11), channel_id=1, source_target_pairs={{0,8},{4,12},{8,16},{12,20},{16,24},{20,28},{24,32},{28,36},{32,40... | collective-permute-start | bytes 73736 | tf_op jit(solution)/shard_map/ppermute | solution.py:51
  97.3 11.7 %collective-permute-start.5 = (bf16[96,128]{1,0:T(8,128)(2,1)S(1)}, bf16[96,128]{1,0:T(8,128)(2,1)S(1)}, u32[]{:S(2)}, u32[]{:S(2)}) collective-permute-start(bf16[96,128]{1,0:T(8,128)(2,1)S(1)} %get-tuple-element.10), channel_id=1, source_target_pairs={{0,4},{4,8},{8,12},{12,16},{16,20},{20,24},{24,28},{28,32},{32,36}... | collective-permute-start | bytes 73736 | tf_op jit(solution)/shard_map/ppermute | solution.py:51
  99.1 10.0 %collective-permute-start.6 = (bf16[96,128]{1,0:T(8,128)(2,1)S(1)}, bf16[96,128]{1,0:T(8,128)(2,1)S(1)}, u32[]{:S(2)}, u32[]{:S(2)}) collective-permute-start(bf16[96,128]{1,0:T(8,128)(2,1)S(1)} %get-tuple-element.9), channel_id=1, source_target_pairs={{0,252},{4,0},{8,4},{12,8},{16,12},{20,16},{24,20},{28,24},{32,28}... | collective-permute-start | bytes 73736 | tf_op jit(solution)/shard_map/ppermute | solution.py:51
  99.1 10.0 %collective-permute-start.7 = (bf16[96,128]{1,0:T(8,128)(2,1)S(1)}, bf16[96,128]{1,0:T(8,128)(2,1)S(1)}, u32[]{:S(2)}, u32[]{:S(2)}) collective-permute-start(bf16[96,128]{1,0:T(8,128)(2,1)S(1)} %get-tuple-element.8), channel_id=1, source_target_pairs={{0,248},{4,252},{8,0},{12,4},{16,8},{20,12},{24,16},{28,20},{32,24... | collective-permute-start | bytes 73736 | tf_op jit(solution)/shard_map/ppermute | solution.py:51
  102.7 11.3 %copy-start.6 = (bf16[512]{0:T(512)(128)(2,1)S(1)}, bf16[512]{0:T(512)(128)(2,1)}, u32[]{:S(2)}) copy-start(bf16[512]{0:T(512)(128)(2,1)} %param.26) | copy-start | bytes 3076
  102.7 11.3 %copy-start.7 = (bf16[512]{0:T(512)(128)(2,1)S(1)}, bf16[512]{0:T(512)(128)(2,1)}, u32[]{:S(2)}) copy-start(bf16[512]{0:T(512)(128)(2,1)} %param.27) | copy-start | bytes 3076
  108.9 9.6 %copy-start.2 = (bf16[80,512]{1,0:T(8,128)(2,1)S(1)}, bf16[80,512]{1,0:T(8,128)(2,1)}, u32[]{:S(2)}) copy-start(bf16[80,512]{1,0:T(8,128)(2,1)} %param.14) | copy-start | bytes 245764
  108.9 9.6 %copy-start.8 = (bf16[512,512]{1,0:T(8,128)(2,1)S(1)}, bf16[512,512]{1,0:T(8,128)(2,1)}, u32[]{:S(2)}) copy-start(bf16[512,512]{1,0:T(8,128)(2,1)} %param.25) | copy-start | bytes 1572868
  110.7 7.8 %all-to-all-start.6 = ((bf16[4,80,128]{2,1,0:T(8,128)(2,1)}), bf16[4,80,128]{2,1,0:T(8,128)(2,1)S(1)}, u32[]{:S(2)}, u32[]{:S(2)}) async-start(bf16[4,80,128]{2,1,0:T(8,128)(2,1)} %bitcast.17), calls=%async_computation.6 | async-start | bytes 163840 | tf_op jit(solution)/shard_map/all_to_all | solution.py:46

commit v2 on v1

v2 whole, which is shorter than its diff:
```python
import functools

import jax
import jax.numpy as jnp
from jax import lax
from jax.experimental import pallas as pl
from jax.experimental.pallas import tpu as pltpu
from jax.sharding import PartitionSpec as P

NODE_DEV = 320
NODE_PAD = 384
SLOT = 96
FAR_SLOT = 16
REACH = 2
OFFSETS = (-2, -1, 1, 2)
LANES = 128
CHUNKS = 4

epsilon = 1e-05

BF16 = jnp.bfloat16
F32 = jnp.float32


def dot(a, b):
    return jnp.dot(a, b, preferred_element_type=F32)


def one_hot(cond):
    return jnp.where(cond, 1.0, 0.0).astype(BF16)


def silu(v):
    return v / (1.0 + jnp.exp(-v))


def layer_norm(outputs, gain, shift):
    average = jnp.mean(outputs, axis=-1, keepdims=True)
    centered = outputs - average
    variance = jnp.mean(centered * centered, axis=-1, keepdims=True)
    return centered * lax.rsqrt(variance + epsilon) * gain + shift


def await_bytes(ref, sem):
    pltpu.make_async_copy(ref, ref, sem).wait()


def step_kernel(
    groups,
    parts,
    node_ref,
    edge_hbm,
    snd_ref,
    ref_ref,
    list_ref,
    cnt_ref,
    w1_hbm,
    w2_hbm,
    eg_ref,
    es_ref,
    nw1_hbm,
    nw2_hbm,
    ng_ref,
    ns_ref,
    out_edges_hbm,
    out_nodes_ref,
    w1,
    w2,
    nw1,
    nw2,
    edges,
    region,
    refs,
    lists,
    lsel,
    lsel_t,
    table,
    outgoing,
    sel,
    sel_t,
    rows_row,
    base,
    picked,
    pieces,
    updated,
    sent,
    msgs,
    acc,
    back_out,
    returned,
    totals,
    agg,
    load_sem,
    f1_send,
    f1_recv,
    fr_send,
    fr_recv,
    far_send,
    far_recv,
    near_send,
    near_recv,
    f3_send,
    f3_recv,
    b1_send,
    b1_recv,
    bfar_send,
    bfar_recv,
    bnear_send,
    bnear_recv,
    b3_send,
    b3_recv,
    store_sem,
):
    own = lax.axis_index("graph")
    share = lax.axis_index("feat")
    far_rows = groups * FAR_SLOT
    table_rows = far_rows + len(OFFSETS) * SLOT
    edge_local = edge_hbm.shape[0]
    width = edge_hbm.shape[1]
    quarter = width // parts
    node_local = node_ref.shape[0]
    ce = edge_local // CHUNKS
    cw = parts * ce

    def graph_peer(i):
        return lax.rem(own + i, groups)

    def feat_peer(j):
        return lax.rem(share + j, parts)

    def near_target(d):
        return lax.rem(own + d + groups, groups)

    barrier = pltpu.get_barrier_semaphore()
    for j in range(1, parts):
        pl.semaphore_signal(barrier, inc=1, device_id={"feat": feat_peer(j)})

    @pl.loop(1, groups)
    def _(i):
        pl.semaphore_signal(barrier, inc=1, device_id={"graph": graph_peer(i)})

    loads = [
        pltpu.make_async_copy(src, dst, load_sem.at[n])
        for n, (src, dst) in enumerate(
            ((edge_hbm, edges), (w1_hbm, w1), (w2_hbm, w2), (nw1_hbm, nw1), (nw2_hbm, nw2))
        )
    ]
    for load in loads:
        load.start()

    lists[...] = jnp.zeros_like(lists)
    lists[: groups, :SLOT] = list_ref[...]
    turned = lists[...].T
    lane = lax.broadcasted_iota(jnp.int32, (FAR_SLOT, NODE_PAD), 1)
    for s in range(groups):
        ids = jnp.broadcast_to(turned[:FAR_SLOT, s : s + 1], (FAR_SLOT, NODE_PAD))
        lsel[s * FAR_SLOT : (s + 1) * FAR_SLOT, :] = one_hot(ids == lane)
    lane = lax.broadcasted_iota(jnp.int32, (SLOT, LANES), 1)
    for n, d in enumerate(OFFSETS):
        ids = lists[pl.ds(near_target(d), 1), :]
        ids = jnp.broadcast_to(ids, (LANES, LANES)).T[:SLOT, :]
        first = far_rows + n * SLOT
        for t in range(NODE_PAD // LANES):
            lsel[first : first + SLOT, t * LANES : (t + 1) * LANES] = one_hot(ids == lane + t * LANES)

    own_block = pl.ds(pl.multiple_of(own * FAR_SLOT, FAR_SLOT), FAR_SLOT)
    table[own_block, :] = jnp.zeros((FAR_SLOT, quarter), BF16)
    returned[own_block, :] = jnp.zeros((FAR_SLOT, quarter), BF16)
    region[NODE_DEV:, :] = jnp.zeros((NODE_PAD - NODE_DEV, width), BF16)
    own_nodes = pl.ds(pl.multiple_of(share * node_local, 16), node_local)
    region[own_nodes, :] = node_ref[...]
    refs[pl.ds(share, 1)] = ref_ref[...][None]

    pl.semaphore_wait(barrier, groups - 1 + parts - 1)

    sends = []
    for j in range(1, parts):
        to = {"feat": feat_peer(j)}
        sends.append(
            pltpu.make_async_remote_copy(
                src_ref=node_ref,
                dst_ref=region.at[own_nodes],
                send_sem=f1_send.at[j],
                recv_sem=f1_recv.at[share],
                device_id=to,
            )
        )
        sends.append(
            pltpu.make_async_remote_copy(
                src_ref=ref_ref,
                dst_ref=refs.at[share],
                send_sem=fr_send.at[j],
                recv_sem=fr_recv.at[share],
                device_id=to,
            )
        )
    for send in sends:
        send.start()
    for j in range(1, parts):
        p = feat_peer(j)
        await_bytes(
            region.at[pl.ds(pl.multiple_of(p * node_local, 16), node_local)], f1_recv.at[p]
        )

    my_lanes = pl.ds(pl.multiple_of(share * quarter, LANES), quarter)
    outgoing[...] = dot(lsel[...], region[:, my_lanes]).astype(BF16)

    def far_copy(i, source, target, send_sem, recv_sem):
        peer = graph_peer(i)
        return pltpu.make_async_remote_copy(
            src_ref=source.at[pl.ds(pl.multiple_of(peer * FAR_SLOT, FAR_SLOT), FAR_SLOT)],
            dst_ref=target.at[own_block],
            send_sem=send_sem,
            recv_sem=recv_sem,
            device_id={"graph": peer},
        )

    def near_copy(n, d, source, target, send_sem, recv_sem):
        block = pl.ds(far_rows + n * SLOT, SLOT)
        return pltpu.make_async_remote_copy(
            src_ref=source.at[block],
            dst_ref=target.at[block],
            send_sem=send_sem.at[n],
            recv_sem=recv_sem.at[n],
            device_id={"graph": near_target(d)},
        )

    near_out = [
        near_copy(n, d, outgoing, table, near_send, near_recv) for n, d in enumerate(OFFSETS)
    ]
    for send in near_out:
        send.start()

    @pl.loop(1, groups)
    def _(i):
        far_copy(i, outgoing, table, far_send, far_recv).start()

    for j in range(1, parts):
        p = feat_peer(j)
        await_bytes(refs.at[p], fr_recv.at[p])
    for p in range(parts):
        value = refs[p]
        offset = jnp.maximum(value - NODE_DEV, 0)
        source = lax.shift_right_logical(offset * 10923, 20)
        slot = offset - source * SLOT
        row = source * FAR_SLOT + slot
        for n, d in enumerate(OFFSETS):
            row = jnp.where(source == near_target(-d), far_rows + n * SLOT + slot, row)
        row = jnp.where(value < NODE_DEV, table_rows + value, row)
        for c in range(CHUNKS):
            first = c * cw + p * ce
            rows_row[:, first : first + ce] = row[:, c * ce : (c + 1) * ce]

    @pl.loop(0, CHUNKS * cw // LANES)
    def _(b):
        at = pl.multiple_of(b * LANES, LANES)
        ids = jnp.broadcast_to(rows_row[:, pl.ds(at, LANES)], (LANES, LANES)).T
        lanes = lax.broadcasted_iota(jnp.int32, (LANES, LANES), 1)
        for t in range(table_rows // LANES):
            sel[pl.ds(at, LANES), t * LANES : (t + 1) * LANES] = one_hot(ids == lanes + t * LANES)

    for load in loads[:2]:
        load.wait()

    block = 64

    @pl.loop(0, (table_rows + NODE_DEV) // block)
    def _(b):
        at = pl.multiple_of(b * block, block)
        for k in range(0, CHUNKS * cw, 512):
            subs = lax.broadcasted_iota(jnp.int32, (block, 512), 0) + at
            ids = jnp.broadcast_to(rows_row[:, k : k + 512], (block, 512))
            sel_t[pl.ds(at, block), k : k + 512] = one_hot(ids == subs)

    @pl.loop(0, edge_local // LANES)
    def _(b):
        at = pl.multiple_of(b * LANES, LANES)
        lanes = lax.broadcasted_iota(jnp.int32, (LANES, LANES), 1)
        rows = []
        for ids_ref in (snd_ref, ref_ref):
            ids = jnp.broadcast_to(ids_ref[:, pl.ds(at, LANES)], (LANES, LANES)).T
            chosen = jnp.concatenate(
                [one_hot(ids == lanes + t * LANES) for t in range(NODE_PAD // LANES)], axis=1
            )
            rows.append(dot(chosen, region[...]).astype(BF16))
        joined = jnp.concatenate([edges[pl.ds(at, LANES), :], *rows], axis=1)
        base[pl.ds(at, LANES), :] = dot(joined, w1[...])

    for t in range(NODE_PAD // LANES):
        for r in range(table_rows // LANES):
            tile = lsel[r * LANES : (r + 1) * LANES, t * LANES : (t + 1) * LANES]
            lsel_t[t * LANES : (t + 1) * LANES, r * LANES : (r + 1) * LANES] = (
                tile.astype(F32).T.astype(BF16)
            )

    for load in loads[2:]:
        load.wait()
    node_base = dot(node_ref[...], nw1[:width, :])

    for n in range(len(OFFSETS)):
        await_bytes(table.at[pl.ds(far_rows + n * SLOT, SLOT)], near_recv.at[n])
    await_bytes(table.at[pl.ds(0, far_rows - FAR_SLOT)], far_recv)

    def rows_for(c, p):
        at = pl.multiple_of(c * cw + p * ce, ce)
        return dot(sel[pl.ds(at, ce), :], table[...]).astype(BF16)

    row_sends = []
    for c in range(CHUNKS):
        for j in (2, 1, 3):
            p = feat_peer(j)
            picked[c, j] = rows_for(c, p)
            send = pltpu.make_async_remote_copy(
                src_ref=picked.at[c, j],
                dst_ref=pieces.at[c, share],
                send_sem=f3_send.at[c, j],
                recv_sem=f3_recv.at[c, share],
                device_id={"feat": p},
            )
            send.start()
            row_sends.append(send)
        pieces[c, pl.ds(share, 1)] = rows_for(c, share)[None]

    gain = eg_ref[...].astype(F32)
    shift = es_ref[...].astype(F32)
    count = cnt_ref[0]
    message_sends = []
    for c in range(CHUNKS):
        for j in range(1, parts):
            p = feat_peer(j)
            await_bytes(pieces.at[c, p], f3_recv.at[c, p])
        at = c * ce
        away = jnp.concatenate([pieces[c, p] for p in range(parts)], axis=1)
        pre = base[at : at + ce, :] + dot(away, w1[2 * width :, :])
        outputs = dot(silu(pre).astype(BF16), w2[...])
        before = edges[at : at + ce, :]
        update = before.astype(F32) + layer_norm(outputs, gain, shift)
        index = lax.broadcasted_iota(jnp.int32, (ce, width), 0) + (share * edge_local + at)
        live = index < count
        fresh = jnp.where(live, update, before.astype(F32))
        updated[at : at + ce, :] = fresh.astype(BF16)
        message = jnp.where(live, fresh, 0.0).astype(BF16)
        for p in range(parts):
            sent[c, p] = message[:, p * quarter : (p + 1) * quarter]
        for j in (2, 1, 3):
            p = feat_peer(j)
            send = pltpu.make_async_remote_copy(
                src_ref=sent.at[c, p],
                dst_ref=msgs.at[c, share],
                send_sem=b1_send.at[c, j],
                recv_sem=b1_recv.at[c, share],
                device_id={"feat": p},
            )
            send.start()
            message_sends.append(send)
        msgs[c, pl.ds(share, 1)] = sent[c, pl.ds(share, 1)]
    store = pltpu.make_async_copy(updated, out_edges_hbm, store_sem)
    store.start()

    for c in range(CHUNKS):
        for j in range(1, parts):
            p = feat_peer(j)
            await_bytes(msgs.at[c, p], b1_recv.at[c, p])
        part = dot(
            sel_t[:, c * cw : (c + 1) * cw], msgs[c].reshape(cw, quarter)
        )
        if c == 0:
            acc[...] = part
        elif c < CHUNKS - 1:
            acc[...] += part
        else:
            part = acc[...] + part
            back_out[...] = part[:table_rows].astype(BF16)
            acc[table_rows:, :] = part[table_rows:]

    def near_return(n, d):
        block = pl.ds(far_rows + n * SLOT, SLOT)
        return pltpu.make_async_remote_copy(
            src_ref=back_out.at[block],
            dst_ref=returned.at[block],
            send_sem=bnear_send.at[n],
            recv_sem=bnear_recv.at[n],
            device_id={"graph": near_target(-d)},
        )

    near_back = [near_return(n, d) for n, d in enumerate(OFFSETS)]
    for send in near_back:
        send.start()

    @pl.loop(1, groups)
    def _(i):
        far_copy(i, back_out, returned, bfar_send, bfar_recv).start()

    for n in range(len(OFFSETS)):
        await_bytes(returned.at[pl.ds(far_rows + n * SLOT, SLOT)], bnear_recv.at[n])
    await_bytes(returned.at[pl.ds(0, far_rows - FAR_SLOT)], bfar_recv)

    totals[...] = (
        acc[table_rows:, :] + dot(lsel_t[...], returned[...])[:NODE_DEV]
    ).astype(BF16)
    total_sends = []
    for j in range(1, parts):
        p = feat_peer(j)
        send = pltpu.make_async_remote_copy(
            src_ref=totals.at[pl.ds(pl.multiple_of(p * node_local, 16), node_local)],
            dst_ref=agg.at[share],
            send_sem=b3_send.at[j],
            recv_sem=b3_recv.at[share],
            device_id={"feat": p},
        )
        send.start()
        total_sends.append(send)
    agg[pl.ds(share, 1)] = totals[own_nodes, :][None]
    for j in range(1, parts):
        p = feat_peer(j)
        await_bytes(agg.at[p], b3_recv.at[p])

    aggregate = jnp.concatenate([agg[p] for p in range(parts)], axis=1)
    pre = node_base + dot(aggregate, nw1[width:, :])
    outputs = dot(silu(pre).astype(BF16), nw2[...])
    out_nodes_ref[...] = (
        node_ref[...].astype(F32)
        + layer_norm(outputs, ng_ref[...].astype(F32), ns_ref[...].astype(F32))
    ).astype(BF16)

    for send in sends + near_out + row_sends + message_sends + near_back + total_sends:
        send.wait_send()
    await_bytes(outgoing.at[pl.ds(0, far_rows - FAR_SLOT)], far_send)
    await_bytes(back_out.at[pl.ds(0, far_rows - FAR_SLOT)], bfar_send)
    store.wait()


def per_device(
    node_feats,
    edge_feats,
    senders,
    receiver_ref,
    send_list,
    edge_count,
    edge_w1,
    edge_w2,
    edge_gain,
    edge_shift,
    node_w1,
    node_w2,
    node_gain,
    node_shift,
):
    groups = lax.axis_size("graph")
    parts = lax.axis_size("feat")
    node_local, width = node_feats.shape
    edge_local = edge_feats.shape[0]
    quarter = width // parts
    far_rows = groups * FAR_SLOT
    table_rows = far_rows + len(OFFSETS) * SLOT
    edge_region = parts * edge_local
    ce = edge_local // CHUNKS
    near = len(OFFSETS)
    vmem = pl.BlockSpec(memory_space=pltpu.VMEM)
    smem = pl.BlockSpec(memory_space=pltpu.SMEM)
    hbm = pl.BlockSpec(memory_space=pl.ANY)
    dma = pltpu.SemaphoreType.DMA
    return pl.pallas_call(
        functools.partial(step_kernel, groups, parts),
        out_shape=(
            jax.ShapeDtypeStruct(edge_feats.shape, BF16),
            jax.ShapeDtypeStruct(node_feats.shape, BF16),
        ),
        in_specs=[
            vmem, hbm, vmem, vmem, vmem, smem, hbm, hbm, vmem, vmem, hbm, hbm, vmem, vmem,
        ],
        out_specs=(hbm, vmem),
        scratch_shapes=[
            pltpu.VMEM(edge_w1.shape, BF16),
            pltpu.VMEM(edge_w2.shape, BF16),
            pltpu.VMEM(node_w1.shape, BF16),
            pltpu.VMEM(node_w2.shape, BF16),
            pltpu.VMEM(edge_feats.shape, BF16),
            pltpu.VMEM((NODE_PAD, width), BF16),
            pltpu.VMEM((parts, 1, edge_local), jnp.int32),
            pltpu.VMEM((LANES, LANES), jnp.int32),
            pltpu.VMEM((table_rows, NODE_PAD), BF16),
            pltpu.VMEM((NODE_PAD, table_rows), BF16),
            pltpu.VMEM((table_rows, quarter), BF16),
            pltpu.VMEM((table_rows, quarter), BF16),
            pltpu.VMEM((edge_region, table_rows), BF16),
            pltpu.VMEM((table_rows + NODE_DEV, edge_region), BF16),
            pltpu.VMEM((1, edge_region), jnp.int32),
            pltpu.VMEM((edge_local, width), F32),
            pltpu.VMEM((CHUNKS, parts, ce, quarter), BF16),
            pltpu.VMEM((CHUNKS, parts, ce, quarter), BF16),
            pltpu.VMEM(edge_feats.shape, BF16),
            pltpu.VMEM((CHUNKS, parts, ce, quarter), BF16),
            pltpu.VMEM((CHUNKS, parts, ce, quarter), BF16),
            pltpu.VMEM((table_rows + NODE_DEV, quarter), F32),
            pltpu.VMEM((table_rows, quarter), BF16),
            pltpu.VMEM((table_rows, quarter), BF16),
            pltpu.VMEM((NODE_DEV, quarter), BF16),
            pltpu.VMEM((parts, node_local, quarter), BF16),
            dma((5,)),
            dma((parts,)),
            dma((parts,)),
            dma((parts,)),
            dma((parts,)),
            dma,
            dma,
            dma((near,)),
            dma((near,)),
            dma((CHUNKS, parts)),
            dma((CHUNKS, parts)),
            dma((CHUNKS, parts)),
            dma((CHUNKS, parts)),
            dma,
            dma,
            dma((near,)),
            dma((near,)),
            dma((parts,)),
            dma((parts,)),
            dma,
        ],
        compiler_params=pltpu.CompilerParams(
            collective_id=0, has_side_effects=True, vmem_limit_bytes=56 * 2**20
        ),
        name="step",
    )(
        node_feats,
        edge_feats,
        senders.reshape(1, -1),
        receiver_ref.reshape(1, -1),
        send_list[0],
        edge_count,
        edge_w1,
        edge_w2,
        edge_gain.reshape(1, -1),
        edge_shift.reshape(1, -1),
        node_w1,
        node_w2,
        node_gain.reshape(1, -1),
        node_shift.reshape(1, -1),
    )


def solution(mesh):
    return jax.shard_map(
        per_device,
        mesh=mesh,
        in_specs=(
            P(("graph", "feat"), None),
            P(("graph", "feat"), None),
            P(("graph", "feat")),
            P(("graph", "feat")),
            P("graph", None, None),
            P("graph"),
            P(),
            P(),
            P(),
            P(),
            P(),
            P(),
            P(),
            P(),
        ),
        out_specs=(P(("graph", "feat"), None), P(("graph", "feat"), None)),
        check_vma=False,
    )
```

time: 122 us -> 71 us (0.58)
  Pallas kernels: 0 us -> 61 us
  starting transfers between devices: 50.7 us -> 0 us
  waiting for transfers between devices: 27.9 us -> 0 us
  matrix products: 17.3 us -> 0 us
  blocking collectives: 10.7 us -> 0 us
  other arithmetic: 3.4 us -> 0 us
  local copies, waits for them, and re-layouts: 9.7 us -> 8.44 us
    pallas_call x0 -> x1, Pallas kernels: none -> 61 us  [per_device(): pl.pallas_call(functools.partial(step_kernel, groups, parts), out_shape=(...]
    all_to_all x6 -> x0, starting transfers between devices: 37.1 us -> none  [exchange(): return lax.all_to_all(tiles, axis, split_axis=0, concat_axis=0, tiled=True)]
    all_to_all x6 -> x0, waiting for transfers between devices: 27.8 us -> none  [exchange(): return lax.all_to_all(tiles, axis, split_axis=0, concat_axis=0, tiled=True)]
    dot_general x9 -> x0, matrix products: 17.3 us -> none  [the longest x3 6.44 us: sum_into(): lax.dot_general(selector, values, (((0,), (0,)), ((), ())), preferred_ele...]
    ppermute x8 -> x0, starting transfers between devices: 13.6 us -> none  [passed_along(): lax.ppermute(value, axis, [(i, (i + by) % devices) for i in range(devices)])]
    all_to_all x1 -> x0, blocking collectives: 10.7 us -> none  [exchange(): return lax.all_to_all(tiles, axis, split_axis=0, concat_axis=0, tiled=True)]
    broadcast_in_dim x2 -> x0, local copies, waits for them, and re-layouts: 3.04 us -> none  [everywhere(): jnp.broadcast_to(value[None], (devices, *value.shape))]
    reshape x3 -> x4, local copies, waits for them, and re-layouts: 2.15 us -> 5.05 us  [the longest x1 1.27 us: per_device(): node_shift.reshape(1, -1)]
  transfers between devices with their start and end apart: 14 -> 0, of which waited for: 7 -> 0; matrix products, arithmetic and copies ran while one was open for 6% -> 0% of each run, Pallas kernels for 0% -> 0%
where the time goes in v2:
time: 71 us; the launch traced here: 70.7 us
  Pallas kernels  61 us (86%)
  local copies, waits for them, and re-layouts  8.44 us (12%)
  between operations  1.29 us (2%)
    pallas_call x1, Pallas kernels, per_device(): pl.pallas_call(functools.partial(step_kernel, groups, parts), out_shape=(...  61 us
    unnamed x2, local copies, waits for them, and re-layouts  3.4 us

profile of v2, /device:TPU:1, one launch (start us, length us, event | category | flops | bytes accessed | tf_op | source)
XLA Modules:
  0.0 70.7 jit_solution(9084100820894540273)
XLA Ops:
  1.3 1.3 %reshape.24.eg_ref = bf16[1,512]{1,0:T(2,128)(2,1)} reshape(bf16[512]{0:T(512)(128)(2,1)} %param.22) | data formatting | bytes 2048 | tf_op jit(solution)/shard_map/reshape | solution.py:534
  2.5 1.3 %reshape.25.es_ref = bf16[1,512]{1,0:T(2,128)(2,1)} reshape(bf16[512]{0:T(512)(128)(2,1)} %param.23) | data formatting | bytes 2048 | tf_op jit(solution)/shard_map/reshape | solution.py:535
  3.8 1.3 %reshape.26.ng_ref = bf16[1,512]{1,0:T(2,128)(2,1)} reshape(bf16[512]{0:T(512)(128)(2,1)} %param.26) | data formatting | bytes 2048 | tf_op jit(solution)/shard_map/reshape | solution.py:538
  5.1 1.3 %reshape.27.ns_ref = bf16[1,512]{1,0:T(2,128)(2,1)} reshape(bf16[512]{0:T(512)(128)(2,1)} %param.27) | data formatting | bytes 2048 | tf_op jit(solution)/shard_map/reshape | solution.py:539
  6.3 61.0 %step.1 = (bf16[512,512]{1,0:T(8,128)(2,1)}, bf16[80,512]{1,0:T(8,128)(2,1)}) custom-call(bf16[80,512]{1,0:T(8,128)(2,1)} %node_ref.1, bf16[512,512]{1,0:T(8,128)(2,1)} %edge_hbm.1, s32[1,512]{1,0:T(1,128)} %bitcast.4, s32[1,512]{1,0:T(1,128)} %bitcast.5, s32[64,96]{1,0:T(8,128)} %bitcast.3, s32[1]{0:T(128)S(6)} %copy.18.cnt_ref, bf16[1536,512]{1,0:T(8,128)(2,1)} %w1_hbm.1, ...), custom_call_target="tpu_custom_call" | custom-call | tf_op jit(solution)/shard_map/step/pallas_call | solution.py:463
  67.3 1.9 %copy.19 = bf16[512,512]{1,0:T(8,128)(2,1)} copy(bf16[512,512]{1,0:T(8,128)(2,1)} %get-tuple-element.4) | data formatting | bytes 1048576
  69.2 1.5 %copy.20 = bf16[80,512]{1,0:T(8,128)(2,1)} copy(bf16[80,512]{1,0:T(8,128)(2,1)} %get-tuple-element.5) | data formatting | bytes 163840

commit v3 on v2

v3 whole, which is shorter than its diff:
```python
import functools

import jax
import jax.numpy as jnp
from jax import lax
from jax.experimental import pallas as pl
from jax.experimental.pallas import tpu as pltpu
from jax.sharding import PartitionSpec as P

NODE_DEV = 320
NODE_PAD = 384
SLOT = 96
FAR_SLOT = 16
REACH = 2
OFFSETS = (-2, -1, 1, 2)
LANES = 128
ROW = 4
PAIR = 2
CHUNKS = 4

epsilon = 1e-05

BF16 = jnp.bfloat16
F32 = jnp.float32


def dot(a, b):
    return jnp.dot(a, b, preferred_element_type=F32)


def one_hot(cond):
    return jnp.where(cond, 1.0, 0.0).astype(BF16)


def silu(v):
    return v / (1.0 + jnp.exp(-v))


def layer_norm(outputs, gain, shift):
    average = jnp.mean(outputs, axis=-1, keepdims=True)
    centered = outputs - average
    variance = jnp.mean(centered * centered, axis=-1, keepdims=True)
    return centered * lax.rsqrt(variance + epsilon) * gain + shift


class Phases:
    def __init__(self):
        self.scope = None

    def __call__(self, name):
        self.end()
        self.scope = jax.named_scope(name)
        self.scope.__enter__()

    def end(self):
        if self.scope is not None:
            self.scope.__exit__(None, None, None)
            self.scope = None


def in_hbm(value):
    return pltpu.with_memory_space_constraint(value, pltpu.HBM)


def await_bytes(ref, sem):
    pltpu.make_async_copy(ref, ref, sem).wait()


def step_kernel(
    groups,
    parts,
    node_hbm,
    edge_hbm,
    snd_hbm,
    ref_hbm,
    list_hbm,
    cnt_ref,
    w1_hbm,
    w2_hbm,
    eg_hbm,
    es_hbm,
    nw1_hbm,
    nw2_hbm,
    ng_hbm,
    ns_hbm,
    new_edges,
    new_nodes,
    nodes,
    edges,
    snd_ref,
    ref_ref,
    list_ref,
    w1,
    w2,
    eg_ref,
    es_ref,
    nw1,
    nw2,
    ng_ref,
    ns_ref,
    region,
    refs,
    lists,
    lsel,
    lsel_t,
    table,
    outgoing,
    sel,
    sel_t,
    rows_row,
    base,
    picked,
    pieces,
    sent,
    msgs,
    acc,
    back_out,
    returned,
    totals,
    agg,
    node_sem,
    load_sem,
    row_in,
    pair_in,
    f1_send,
    f1_recv,
    fr_send,
    fr_recv,
    f2_send,
    f2_recv,
    f3_send,
    f3_recv,
    b1_send,
    b1_recv,
    b2_send,
    b2_recv,
    b3_send,
    b3_recv,
):
    own = lax.axis_index("graph")
    share = lax.axis_index("feat")
    far_rows = groups * FAR_SLOT
    table_rows = far_rows + len(OFFSETS) * SLOT
    edge_local = edge_hbm.shape[0]
    width = edge_hbm.shape[1]
    quarter = width // parts
    node_local = node_hbm.shape[0]
    ce = edge_local // CHUNKS
    cw = parts * ce

    def graph_peer(i):
        return lax.rem(own + i, groups)

    def feat_peer(j):
        return lax.rem(share + j, parts)

    def near_target(d):
        return lax.rem(own + d + groups, groups)

    place = lax.rem(own, ROW * PAIR)
    core = lax.rem(own, PAIR)
    pair_peer = own + 1 - 2 * core

    def row_peer(i):
        return own - place + lax.rem(place + i * PAIR, ROW * PAIR)

    phase = Phases()
    phase("signal")
    barrier = pltpu.get_barrier_semaphore()
    line = groups // (ROW * PAIR)
    for i in sorted(range(1, line), key=lambda z: -min(z, line - z)):
        at = lax.rem(own + i * ROW * PAIR, groups)
        pl.semaphore_signal(barrier, inc=1, device_id={"graph": at})
    for j in range(1, parts):
        pl.semaphore_signal(barrier, inc=1, device_id={"feat": feat_peer(j)})
    for i in range(1, ROW):
        pl.semaphore_signal(barrier, inc=1, device_id={"graph": row_peer(i)})
    pl.semaphore_signal(barrier, inc=1, device_id={"graph": pair_peer})
    for p in range(parts):
        pltpu.make_async_copy(
            node_hbm.at[:, p * quarter : (p + 1) * quarter], nodes.at[p], node_sem
        ).start()
    loads = [
        pltpu.make_async_copy(src, dst, load_sem.at[n])
        for n, (src, dst) in enumerate(
            (
                (ref_hbm, ref_ref),
                (list_hbm, list_ref),
                (snd_hbm, snd_ref),
                (edge_hbm, edges),
                (w1_hbm, w1),
                (w2_hbm, w2),
                (eg_hbm, eg_ref),
                (es_hbm, es_ref),
                (nw1_hbm, nw1),
                (nw2_hbm, nw2),
                (ng_hbm, ng_ref),
                (ns_hbm, ns_ref),
            )
        )
    ]
    for load in loads[:2]:
        load.start()

    phase("prep")
    own_block = pl.ds(pl.multiple_of(own * FAR_SLOT, FAR_SLOT), FAR_SLOT)
    table[own_block, :] = jnp.zeros((FAR_SLOT, quarter), BF16)
    returned[own_block, :] = jnp.zeros((FAR_SLOT, quarter), BF16)
    region[:, NODE_DEV:, :] = jnp.zeros((parts, NODE_PAD - NODE_DEV, quarter), BF16)
    own_nodes = pl.ds(pl.multiple_of(share * node_local, 16), node_local)
    loads[0].wait()
    await_bytes(nodes, node_sem)
    region[:, own_nodes, :] = nodes[...]
    refs[pl.ds(share, 1)] = ref_ref[...][None]

    phase("barrier")
    pl.semaphore_wait(barrier, line - 1 + parts - 1 + ROW - 1 + 1)

    sends = []
    for j in (2, 1, 3):
        p = feat_peer(j)
        sends.append(
            pltpu.make_async_remote_copy(
                src_ref=nodes.at[p],
                dst_ref=region.at[p, own_nodes],
                send_sem=f1_send,
                recv_sem=f1_recv.at[0],
                device_id={"feat": p},
            )
        )
    for j in (2, 1, 3):
        p = feat_peer(j)
        sends.append(
            pltpu.make_async_remote_copy(
                src_ref=ref_ref,
                dst_ref=refs.at[share],
                send_sem=fr_send,
                recv_sem=fr_recv,
                device_id={"feat": p},
            )
        )
    for send in sends:
        send.start()

    for load in loads[2:]:
        load.start()

    for i in range(1, ROW):
        pl.semaphore_signal(row_in, inc=1, device_id={"graph": row_peer(i)})

    phase("lists")
    lists[...] = jnp.zeros_like(lists)
    loads[1].wait()
    lists[: groups, :SLOT] = list_ref[...]
    turned = lists[...].T
    lane = lax.broadcasted_iota(jnp.int32, (FAR_SLOT, NODE_PAD), 1)
    for s in range(groups):
        ids = jnp.broadcast_to(turned[:FAR_SLOT, s : s + 1], (FAR_SLOT, NODE_PAD))
        lsel[s * FAR_SLOT : (s + 1) * FAR_SLOT, :] = one_hot(ids == lane)
    lane = lax.broadcasted_iota(jnp.int32, (SLOT, LANES), 1)
    for n, d in enumerate(OFFSETS):
        ids = lists[pl.ds(near_target(d), 1), :]
        ids = jnp.broadcast_to(ids, (LANES, LANES)).T[:SLOT, :]
        first = far_rows + n * SLOT
        for t in range(NODE_PAD // LANES):
            lsel[first : first + SLOT, t * LANES : (t + 1) * LANES] = one_hot(ids == lane + t * LANES)

    phase("rows_in")
    pl.semaphore_wait(row_in, ROW - 1)
    pl.semaphore_signal(pair_in, inc=1, device_id={"graph": pair_peer})
    pl.semaphore_wait(pair_in, 1)

    phase("f1_wait")

    others = pl.ds(0, (parts - 1) * node_local)
    await_bytes(region.at[0, others], f1_recv.at[0])

    phase("list_dot")
    outgoing[...] = dot(lsel[...], region[share]).astype(BF16)

    def exchange(source, target, sign, send_sem, recv_sem):
        def far(i):
            peer = graph_peer(i)
            return pltpu.make_async_remote_copy(
                src_ref=source.at[pl.ds(pl.multiple_of(peer * FAR_SLOT, FAR_SLOT), FAR_SLOT)],
                dst_ref=target.at[own_block],
                send_sem=send_sem,
                recv_sem=recv_sem,
                device_id={"graph": peer},
            )

        def send_far():
            plane = ROW * PAIR
            for dz in sorted(range(line), key=lambda z: -min(z, line - z)):
                first = dz * plane + (dz == 0)

                @pl.loop(first, (dz + 1) * plane, unroll=True)
                def _(i):
                    far(i).start()

        def send_near():
            for n, d in enumerate(OFFSETS):
                block = pl.ds(far_rows + n * SLOT, SLOT)
                pltpu.make_async_remote_copy(
                    src_ref=source.at[block],
                    dst_ref=target.at[block],
                    send_sem=send_sem,
                    recv_sem=recv_sem,
                    device_id={"graph": near_target(sign * d)},
                ).start()

        return send_far, send_near

    passed = pl.ds(0, table_rows - FAR_SLOT)
    phase("f2_start")
    for send in exchange(outgoing, table, 1, f2_send, f2_recv):
        send()

    for i in range(1, parts):
        for j in (2, 1, 3):
            p = feat_peer(j)
            q = lax.rem(p + i, parts)
            pltpu.make_async_remote_copy(
                src_ref=nodes.at[q],
                dst_ref=region.at[q, own_nodes],
                send_sem=f1_send,
                recv_sem=f1_recv.at[1],
                device_id={"feat": p},
            ).start()

    await_bytes(refs.at[pl.ds(0, parts - 1)], fr_recv)
    for p in range(parts):
        value = refs[p]
        offset = jnp.maximum(value - NODE_DEV, 0)
        source = lax.shift_right_logical(offset * 10923, 20)
        slot = offset - source * SLOT
        row = source * FAR_SLOT + slot
        for n, d in enumerate(OFFSETS):
            row = jnp.where(source == near_target(-d), far_rows + n * SLOT + slot, row)
        row = jnp.where(value < NODE_DEV, table_rows + value, row)
        for c in range(CHUNKS):
            first = c * cw + p * ce
            rows_row[:, first : first + ce] = row[:, c * ce : (c + 1) * ce]

    phase("sel")
    @pl.loop(0, CHUNKS * cw // LANES)
    def _(b):
        at = pl.multiple_of(b * LANES, LANES)
        ids = jnp.broadcast_to(rows_row[:, pl.ds(at, LANES)], (LANES, LANES)).T
        lanes = lax.broadcasted_iota(jnp.int32, (LANES, LANES), 1)
        for t in range(table_rows // LANES):
            sel[pl.ds(at, LANES), t * LANES : (t + 1) * LANES] = one_hot(ids == lanes + t * LANES)

    phase("load_wait")
    for load in loads[2:5]:
        load.wait()

    phase("sel_t")
    block = 64

    @pl.loop(0, (table_rows + NODE_DEV) // block)
    def _(b):
        at = pl.multiple_of(b * block, block)
        for k in range(0, CHUNKS * cw, 512):
            subs = lax.broadcasted_iota(jnp.int32, (block, 512), 0) + at
            ids = jnp.broadcast_to(rows_row[:, k : k + 512], (block, 512))
            sel_t[pl.ds(at, block), k : k + 512] = one_hot(ids == subs)

    phase("f1b_wait")
    await_bytes(region.at[pl.ds(0, parts - 1), others], f1_recv.at[1])
    phase("base")
    @pl.loop(0, edge_local // LANES)
    def _(b):
        at = pl.multiple_of(b * LANES, LANES)
        lanes = lax.broadcasted_iota(jnp.int32, (LANES, LANES), 1)
        rows = []
        for ids_ref in (snd_ref, ref_ref):
            ids = jnp.broadcast_to(ids_ref[:, pl.ds(at, LANES)], (LANES, LANES)).T
            chosen = jnp.concatenate(
                [one_hot(ids == lanes + t * LANES) for t in range(NODE_PAD // LANES)], axis=1
            )
            whole = jnp.concatenate([region[p] for p in range(parts)], axis=1)
            rows.append(dot(chosen, whole).astype(BF16))
        joined = jnp.concatenate([edges[pl.ds(at, LANES), :], *rows], axis=1)
        base[pl.ds(at, LANES), :] = dot(joined, w1[...])

    for load in loads[5:8]:
        load.wait()

    phase("f2_wait")
    await_bytes(table.at[passed], f2_recv)
    phase("pick")
    def send_rows(c, p):
        pltpu.make_async_remote_copy(
            src_ref=picked.at[c, p],
            dst_ref=pieces.at[c, share],
            send_sem=f3_send,
            recv_sem=f3_recv.at[c],
            device_id={"feat": p},
        ).start()

    for j in (2, 1, 3, 0):
        p = feat_peer(j)
        at = pl.ds(pl.multiple_of(p * ce, ce), ce)
        picked[0, pl.ds(p, 1)] = dot(sel[at, :], table[...]).astype(BF16)[None]
        if j:
            send_rows(0, p)
    for c in range(1, CHUNKS):
        picked[c] = (
            dot(sel[c * cw : (c + 1) * cw, :], table[...]).astype(BF16).reshape(parts, ce, quarter)
        )
        for j in (2, 1, 3):
            send_rows(c, feat_peer(j))
    pieces[:, pl.ds(share, 1)] = picked[:, pl.ds(share, 1)]

    gain = eg_ref[...].astype(F32)[None]
    shift = es_ref[...].astype(F32)[None]
    count = cnt_ref[0]
    for c in range(CHUNKS):
        phase("f3_wait")
        await_bytes(pieces.at[c, pl.ds(0, parts - 1)], f3_recv.at[c])
        phase("mlp")
        at = c * ce
        away = jnp.concatenate([pieces[c, p] for p in range(parts)], axis=1)
        pre = base[at : at + ce, :] + dot(away, w1[2 * width :, :])
        outputs = dot(silu(pre).astype(BF16), w2[...])
        before = edges[at : at + ce, :]
        update = before.astype(F32) + layer_norm(outputs, gain, shift)
        index = lax.broadcasted_iota(jnp.int32, (ce, width), 0) + (share * edge_local + at)
        live = index < count
        new_edges[at : at + ce, :] = jnp.where(live, update, before.astype(F32)).astype(BF16)
        message = jnp.where(live, update, 0.0).astype(BF16)
        for p in range(parts):
            sent[c, p] = message[:, p * quarter : (p + 1) * quarter]
        for j in (2, 1, 3):
            p = feat_peer(j)
            pltpu.make_async_remote_copy(
                src_ref=sent.at[c, p],
                dst_ref=msgs.at[c, share],
                send_sem=b1_send,
                recv_sem=b1_recv.at[c],
                device_id={"feat": p},
            ).start()
        msgs[c, pl.ds(share, 1)] = sent[c, pl.ds(share, 1)]

    for c in range(CHUNKS):
        phase("b1_wait")
        await_bytes(msgs.at[c, pl.ds(0, parts - 1)], b1_recv.at[c])
        phase("seg_sum")
        columns = slice(c * cw, (c + 1) * cw)
        message = msgs[c].reshape(cw, quarter)
        if c == 0:
            acc[...] = dot(sel_t[:, columns], message)
        elif c < CHUNKS - 1:
            acc[...] += dot(sel_t[:, columns], message)

    send_far, send_near = exchange(back_out, returned, -1, b2_send, b2_recv)
    back_out[:far_rows] = (acc[:far_rows] + dot(sel_t[:far_rows, columns], message)).astype(BF16)
    phase("b2_start")
    send_far()
    rest = acc[far_rows:] + dot(sel_t[far_rows:, columns], message)
    back_out[far_rows:] = rest[: table_rows - far_rows].astype(BF16)
    acc[table_rows:, :] = rest[table_rows - far_rows :]
    send_near()
    phase("lsel_t")
    for t in range(NODE_PAD // LANES):
        for r in range(table_rows // LANES):
            tile = lsel[r * LANES : (r + 1) * LANES, t * LANES : (t + 1) * LANES]
            lsel_t[t * LANES : (t + 1) * LANES, r * LANES : (r + 1) * LANES] = (
                tile.astype(F32).T.astype(BF16)
            )

    phase("node_base")
    for load in loads[8:]:
        load.wait()
    own_feats = jnp.concatenate([nodes[p] for p in range(parts)], axis=1)
    node_base = dot(own_feats, nw1[:width, :])

    phase("b2_wait")
    await_bytes(returned.at[passed], b2_recv)

    phase("totals")
    totals[...] = (
        acc[table_rows:, :] + dot(lsel_t[...], returned[...])[:NODE_DEV]
    ).astype(BF16)
    for j in range(1, parts):
        p = feat_peer(j)
        pltpu.make_async_remote_copy(
            src_ref=totals.at[pl.ds(pl.multiple_of(p * node_local, 16), node_local)],
            dst_ref=agg.at[share],
            send_sem=b3_send,
            recv_sem=b3_recv,
            device_id={"feat": p},
        ).start()
    agg[pl.ds(share, 1)] = totals[own_nodes, :][None]
    phase("b3_wait")
    await_bytes(agg.at[pl.ds(0, parts - 1)], b3_recv)

    phase("node")
    aggregate = jnp.concatenate([agg[p] for p in range(parts)], axis=1)
    pre = node_base + dot(aggregate, nw1[width:, :])
    outputs = dot(silu(pre).astype(BF16), nw2[...])
    update = own_feats.astype(F32) + layer_norm(
        outputs, ng_ref[...].astype(F32)[None], ns_ref[...].astype(F32)[None]
    )
    new_nodes[...] = update.astype(BF16)

    phase("drain")
    await_bytes(refs.at[pl.ds(0, parts - 1)], fr_send)
    await_bytes(region.at[:, others], f1_send)
    await_bytes(outgoing.at[passed], f2_send)
    await_bytes(picked.at[:, pl.ds(0, parts - 1)], f3_send)
    await_bytes(sent.at[:, pl.ds(0, parts - 1)], b1_send)
    await_bytes(back_out.at[passed], b2_send)
    await_bytes(agg.at[pl.ds(0, parts - 1)], b3_send)
    phase.end()


def hand_out(edges, nodes, edges_out, nodes_out, edge_sem, node_sem):
    copies = (
        pltpu.make_async_copy(edges, edges_out, edge_sem),
        pltpu.make_async_copy(nodes, nodes_out, node_sem),
    )
    for copy in copies:
        copy.start()
    for copy in copies:
        copy.wait()


def per_device(
    node_feats,
    edge_feats,
    senders,
    receiver_ref,
    send_list,
    edge_count,
    edge_w1,
    edge_w2,
    edge_gain,
    edge_shift,
    node_w1,
    node_w2,
    node_gain,
    node_shift,
):
    groups = lax.axis_size("graph")
    parts = lax.axis_size("feat")
    node_local, width = node_feats.shape
    edge_local = edge_feats.shape[0]
    quarter = width // parts
    far_rows = groups * FAR_SLOT
    table_rows = far_rows + len(OFFSETS) * SLOT
    edge_region = parts * edge_local
    ce = edge_local // CHUNKS
    vmem = pl.BlockSpec(memory_space=pltpu.VMEM)
    smem = pl.BlockSpec(memory_space=pltpu.SMEM)
    hbm = pl.BlockSpec(memory_space=pltpu.HBM)
    dma = pltpu.SemaphoreType.DMA
    finished = pl.pallas_call(
        functools.partial(step_kernel, groups, parts),
        out_shape=(
            pltpu.VMEM(edge_feats.shape, BF16),
            pltpu.VMEM(node_feats.shape, BF16),
        ),
        in_specs=[
            hbm, hbm, hbm, hbm, hbm, smem, hbm, hbm, hbm, hbm, hbm, hbm, hbm, hbm,
        ],
        out_specs=(vmem, vmem),
        scratch_shapes=[
            pltpu.VMEM((parts, node_local, quarter), BF16),
            pltpu.VMEM(edge_feats.shape, BF16),
            pltpu.VMEM((1, edge_local), jnp.int32),
            pltpu.VMEM((1, edge_local), jnp.int32),
            pltpu.VMEM((groups, SLOT), jnp.int32),
            pltpu.VMEM(edge_w1.shape, BF16),
            pltpu.VMEM(edge_w2.shape, BF16),
            pltpu.VMEM((width,), BF16),
            pltpu.VMEM((width,), BF16),
            pltpu.VMEM(node_w1.shape, BF16),
            pltpu.VMEM(node_w2.shape, BF16),
            pltpu.VMEM((width,), BF16),
            pltpu.VMEM((width,), BF16),
            pltpu.VMEM((parts, NODE_PAD, quarter), BF16),
            pltpu.VMEM((parts, 1, edge_local), jnp.int32),
            pltpu.VMEM((LANES, LANES), jnp.int32),
            pltpu.VMEM((table_rows, NODE_PAD), BF16),
            pltpu.VMEM((NODE_PAD, table_rows), BF16),
            pltpu.VMEM((table_rows, quarter), BF16),
            pltpu.VMEM((table_rows, quarter), BF16),
            pltpu.VMEM((edge_region, table_rows), BF16),
            pltpu.VMEM((table_rows + NODE_DEV, edge_region), BF16),
            pltpu.VMEM((1, edge_region), jnp.int32),
            pltpu.VMEM((edge_local, width), F32),
            pltpu.VMEM((CHUNKS, parts, ce, quarter), BF16),
            pltpu.VMEM((CHUNKS, parts, ce, quarter), BF16),
            pltpu.VMEM((CHUNKS, parts, ce, quarter), BF16),
            pltpu.VMEM((CHUNKS, parts, ce, quarter), BF16),
            pltpu.VMEM((table_rows + NODE_DEV, quarter), F32),
            pltpu.VMEM((table_rows, quarter), BF16),
            pltpu.VMEM((table_rows, quarter), BF16),
            pltpu.VMEM((NODE_DEV, quarter), BF16),
            pltpu.VMEM((parts, node_local, quarter), BF16),
            dma,
            dma((12,)),
            pltpu.SemaphoreType.REGULAR,
            pltpu.SemaphoreType.REGULAR,
            dma,
            dma((2,)),
            dma,
            dma,
            dma,
            dma,
            dma,
            dma((CHUNKS,)),
            dma,
            dma((CHUNKS,)),
            dma,
            dma,
            dma,
            dma,
        ],
        compiler_params=pltpu.CompilerParams(
            collective_id=0, has_side_effects=True, vmem_limit_bytes=48 * 2**20
        ),
        name="step",
    )(
        in_hbm(node_feats),
        in_hbm(edge_feats),
        in_hbm(senders.reshape(1, -1)),
        in_hbm(receiver_ref.reshape(1, -1)),
        in_hbm(send_list[0]),
        edge_count,
        in_hbm(edge_w1),
        in_hbm(edge_w2),
        in_hbm(edge_gain),
        in_hbm(edge_shift),
        in_hbm(node_w1),
        in_hbm(node_w2),
        in_hbm(node_gain),
        in_hbm(node_shift),
    )
    return pl.pallas_call(
        hand_out,
        out_shape=(
            jax.ShapeDtypeStruct(edge_feats.shape, BF16),
            jax.ShapeDtypeStruct(node_feats.shape, BF16),
        ),
        in_specs=[vmem, vmem],
        out_specs=(hbm, hbm),
        scratch_shapes=[dma, dma],
        compiler_params=pltpu.CompilerParams(vmem_limit_bytes=2**20),
        name="hand_out",
    )(*(pltpu.with_memory_space_constraint(value, pltpu.VMEM) for value in finished))


def solution(mesh):
    return jax.shard_map(
        per_device,
        mesh=mesh,
        in_specs=(
            P(("graph", "feat"), None),
            P(("graph", "feat"), None),
            P(("graph", "feat")),
            P(("graph", "feat")),
            P("graph", None, None),
            P("graph"),
            P(),
            P(),
            P(),
            P(),
            P(),
            P(),
            P(),
            P(),
        ),
        out_specs=(P(("graph", "feat"), None), P(("graph", "feat"), None)),
        check_vma=False,
    )
```

time: 71 us -> 53.7 us (0.76)
  Pallas kernels: 61 us -> 52.3 us
  local copies, waits for them, and re-layouts: 8.44 us -> 0 us
    pallas_call x1, Pallas kernels: 61 us -> 51.5 us  [per_device(): pl.pallas_call(functools.partial(step_kernel, groups, parts), out_shape=(...]
    reshape x4 -> x0, local copies, waits for them, and re-layouts: 5.05 us -> none  [the longest x1 1.27 us: per_device(): node_shift.reshape(1, -1)]
    unnamed x2 -> x0, local copies, waits for them, and re-layouts: 3.4 us -> none
    pallas_call x0 -> x1, Pallas kernels: none -> 0.83 us  [per_device(): pl.pallas_call(hand_out, out_shape=(jax.ShapeDtypeStruct(edge_feats.shape...]
where the time goes in v3:
time: 53.7 us; the launch traced here: 53.6 us
  Pallas kernels  52.3 us (97%)
  between operations  1.29 us (2%)
    pallas_call x1, Pallas kernels, per_device(): pl.pallas_call(functools.partial(step_kernel, groups, parts), out_shape=(...  51.5 us

profile of v3, /device:TPU:1, one launch (start us, length us, event | category | flops | bytes accessed | tf_op | source)
XLA Modules:
  0.0 53.6 jit_solution(319010188001522562)
XLA Ops:
  1.3 51.5 %step.1 = (bf16[512,512]{1,0:T(8,128)(2,1)S(1)}, bf16[80,512]{1,0:T(8,128)(2,1)S(1)}) custom-call(bf16[80,512]{1,0:T(8,128)(2,1)} %node_hbm.1, bf16[512,512]{1,0:T(8,128)(2,1)} %edge_hbm.1, s32[1,512]{1,0:T(1,128)} %bitcast.4, s32[1,512]{1,0:T(1,128)} %bitcast.5, s32[64,96]{1,0:T(8,128)} %bitcast.3, s32[1]{0:T(128)S(6)} %copy.16.cnt_ref, ...), custom_call_target="tpu_custom_call" | custom-call | tf_op jit(solution)/shard_map/step/pallas_call | solution.py:559
  52.8 0.8 %hand_out.1 = (bf16[512,512]{1,0:T(8,128)(2,1)}, bf16[80,512]{1,0:T(8,128)(2,1)}) custom-call(bf16[512,512]{1,0:T(8,128)(2,1)S(1)} %get-tuple-element.4.edges, bf16[80,512]{1,0:T(8,128)(2,1)S(1)} %get-tuple-element.5.nodes), custom_call_target="tpu_custom_call" | custom-call | tf_op jit(solution)/shard_map/hand_out/pallas_call | solution.py:642
